TPU v7x, 16 devices: a 4x2x1 block of a 4x4x8 slice. The times are simulated.
16 devices in a mesh: rep: 4 (over y, z, core), dp: 4 (over x).
Axes of the slice: x: 4, y: 2, z: 1, core: 2. Of those that a mesh axis runs over, the one named last changes fastest.
The devices are a block of a 4x4x8 slice.
Arguments:
- x: bfloat16 [16, 4096, 768], P(('rep', 'dp')), parts along dimension 0
- dy: bfloat16 [16, 4096, 768], P(('rep', 'dp')), parts along dimension 0
- w_gate: bfloat16 [2, 768, 1792], replicated
- w_up: bfloat16 [2, 768, 1792], replicated
- w_down: bfloat16 [2, 1792, 768], replicated
- m_w_gate: float32 [2, 768, 1792], P(None, 'dp')
- m_w_up: float32 [2, 768, 1792], P(None, 'dp')
- m_w_down: float32 [2, 1792, 768], P(None, 'dp')
- v_w_gate: float32 [2, 768, 1792], P(None, 'dp')
- v_w_up: float32 [2, 768, 1792], P(None, 'dp')
- v_w_down: float32 [2, 1792, 768], P(None, 'dp')
Outputs:
- output 1: bfloat16 [8, 768, 1792], P('rep'), parts along dimension 0
- output 2: bfloat16 [8, 768, 1792], P('rep'), parts along dimension 0
- output 3: bfloat16 [8, 1792, 768], P('rep'), parts along dimension 0
- output 4: float32 [8, 768, 1792], P('rep', 'dp'), parts along dimension 0
- output 5: float32 [8, 768, 1792], P('rep', 'dp'), parts along dimension 0
- output 6: float32 [8, 1792, 768], P('rep', 'dp'), parts along dimension 0
- output 7: float32 [8, 768, 1792], P('rep', 'dp'), parts along dimension 0
- output 8: float32 [8, 768, 1792], P('rep', 'dp'), parts along dimension 0
- output 9: float32 [8, 1792, 768], P('rep', 'dp'), parts along dimension 0
There are 4 independent parts. A program takes and returns all parts, laid end to end along the dimension named above; an argument that names none is the same for every part.
All inputs are finite; a program needn't handle non-finite values.
Results may differ from a plain program's by a relative error of at most 0.022.
Values are sent between devices in bfloat16 or wider.
A program may use at most 768 MiB of HBM per device.

v0:
```python
import jax
import jax.numpy as jnp
from jax import lax

NAMES = ("w_gate", "w_up", "w_down")


def matmul(a, w):
    return jnp.dot(a, w, preferred_element_type=jnp.float32).astype(jnp.bfloat16)


def normed(h):
    wide = h.astype(jnp.float32)
    scale = lax.rsqrt(jnp.mean(wide**2, -1, keepdims=True) + 1e-6)
    return (wide * scale).astype(jnp.bfloat16)


def layer(h, w):
    a = normed(h)
    gate = jnp.dot(a, w["w_gate"], preferred_element_type=jnp.float32)
    up = jnp.dot(a, w["w_up"], preferred_element_type=jnp.float32)
    return h + matmul((jax.nn.silu(gate) * up).astype(jnp.bfloat16), w["w_down"])


def adamw(w, m, v, g):
    m = 0.9 * m + 0.1 * g
    v = 0.95 * v + 0.05 * g * g
    step = m * lax.rsqrt(v + 1e-8) + 0.1 * w
    return (w - 0.02 * step).astype(jnp.bfloat16), m, v


def clipped(gradients, sum_of_squares, count):
    factor = jnp.minimum(1.0, 0.5 * lax.rsqrt(sum_of_squares / count + 1e-30))
    return [g * factor for g in gradients]


def stack(weights, h):
    for number in range(weights["w_gate"].shape[0]):
        h = layer(h, {name: w[number] for name, w in weights.items()})
    return h


def solution(mesh):
    groups = mesh.shape["rep"]

    def step(x, dy, *arrays):
        weights, m, v = (arrays[i : i + 3] for i in (0, 3, 6))
        x, dy = (t.reshape(groups, -1, *t.shape[1:]) for t in (x, dy))

        def of_a_group(x, dy):
            _, back = jax.vjp(lambda w: stack(w, x), dict(zip(NAMES, weights, strict=True)))
            by_weights = back(dy)[0]
            gradients = [by_weights[name].astype(jnp.float32) for name in NAMES]
            gradients = clipped(gradients, sum(jnp.sum(g * g) for g in gradients), sum(g.size for g in gradients))
            new = [adamw(w.astype(jnp.float32), m, v, g) for w, m, v, g in zip(weights, m, v, gradients, strict=True)]
            return tuple(one[which] for which in range(3) for one in new)

        return tuple(t.reshape(-1, *t.shape[2:]) for t in jax.vmap(of_a_group)(x, dy))

    return step
```

profile of v0, /device:TPU:112, one launch (start us, length us, event | category | flops | bytes accessed | tf_op | source)
XLA Modules:
  0.0 782.5 jit_solution(7875363948693304230)
XLA Ops:
  7.2 0.1 reduce-scatter.27.cloned.1.call-start
  7.3 4.1 fusion.35
  11.4 8.8 %copy = bf16[1,4096,768]{1,2,0:T(8,128)(2,1)} copy(bf16[1,4096,768]{2,1,0:T(8,128)(2,1)} %param.2) | data formatting | bytes 12582912 | tf_op args[0]
  20.2 20.0 %fusion.123 = f32[4096,1792]{1,0:T(8,128)} fusion(bf16[2,768,1792]{2,1,0:T(8,128)(2,1)} %param, bf16[1,4096,768]{2,1,0:T(8,128)(2,1)} %param.2, f32[4096]{0:T(1024)S(1)} %add_rsqrt_fusion), kind=kOutput, calls=%fused_computation.132 | convolution fusion | flops 11283726336 | bytes 38420480 | tf_op jit(solution)/vmap(jvp())/dot_general | solution.py:20
  40.2 17.0 %fusion.121 = f32[4096,1792]{1,0:T(8,128)} fusion(bf16[2,768,1792]{2,1,0:T(8,128)(2,1)} %param.3, bf16[1,4096,768]{2,1,0:T(8,128)(2,1)S(1)} %bitcast.360, f32[4096]{0:T(1024)S(1)} %add_rsqrt_fusion), kind=kOutput, calls=%fused_computation.130 | convolution fusion | flops 11283726336 | bytes 38420480 | tf_op jit(solution)/vmap(jvp())/dot_general | solution.py:21
  57.2 25.4 %fusion.26 = bf16[4096,1792]{1,0:T(8,128)(2,1)} fusion(f32[4096,1792]{1,0:T(8,128)} %fusion.121, f32[4096,1792]{1,0:T(8,128)} %fusion.123), kind=kLoop, calls=%fused_computation.44 | loop fusion | flops 44040192 | bytes 73400320
  82.6 19.4 %fusion.39 = (f32[4096]{0:T(1024)S(1)}, bf16[1,1,4096,768]{2,3,1,0:T(8,128)(2,1)}) fusion(bf16[4096,1792]{1,0:T(8,128)(2,1)} %fusion.26, bf16[2,1792,768]{2,1,0:T(8,128)(2,1)} %param.4, bf16[1,4096,768]{1,2,0:T(8,128)(2,1)} %copy), kind=kOutput, calls=%fused_computation.56 | convolution fusion | flops 11290013696 | bytes 30031872 | tf_op jit(solution)/vmap(jvp())/dot_general | solution.py:9
  102.1 0.6 copy-done.5
  102.7 20.4 %fusion.58 = f32[4096,1792]{1,0:T(8,128)} fusion(bf16[1,1,4096,768]{2,3,1,0:T(8,128)(2,1)} %get-tuple-element.10, f32[4096]{0:T(1024)S(1)} %bitcast.369, bf16[2,768,1792]{2,1,0:T(8,128)(2,1)} %param), kind=kOutput, calls=%fused_computation.75 | convolution fusion | flops 11283726336 | bytes 38420480 | tf_op jit(solution)/vmap(jvp())/dot_general | solution.py:20
  123.0 17.0 %fusion.60 = f32[4096,1792]{1,0:T(8,128)} fusion(bf16[1,1,4096,768]{2,3,1,0:T(8,128)(2,1)S(1)} %copy-done.1, f32[4096]{0:T(1024)S(1)} %bitcast.370, bf16[2,768,1792]{2,1,0:T(8,128)(2,1)} %param.3), kind=kOutput, calls=%fused_computation.76 | convolution fusion | flops 11283726336 | bytes 38420480 | tf_op jit(solution)/vmap(jvp())/dot_general | solution.py:21
  140.1 26.6 %fusion.64 = f32[1,1792,768]{2,1,0:T(8,128)} fusion(bf16[1,4096,768]{2,1,0:T(8,128)(2,1)} %param.5, f32[4096,1792]{1,0:T(8,128)} %fusion.60, f32[4096,1792]{1,0:T(8,128)} %fusion.58), kind=kOutput, calls=%fused_computation.78 | convolution fusion | flops 11318329344 | bytes 70516736 | tf_op jit(solution)/vmap(transpose(jvp()))/dot_general | solution.py:9
  166.7 0.1 reduce-scatter.27.cloned.1.call-update
  166.8 0.1 reduce-scatter.29.cloned.1.call-start
  166.8 8.7 %copy.1 = bf16[1,4096,768]{1,2,0:T(8,128)(2,1)} copy(bf16[1,4096,768]{2,1,0:T(8,128)(2,1)} %param.5) | data formatting | bytes 12582912 | tf_op args[1]
  175.5 17.5 %convolution_convert_fusion.1 = bf16[4096,1792]{1,0:T(8,128)(2,1)} fusion(bf16[1,4096,768]{2,1,0:T(8,128)(2,1)} %param.5, bf16[2,1792,768]{2,1,0:T(8,128)(2,1)} %param.4), kind=kOutput, calls=%fused_computation.43 | convolution fusion | flops 11281629184 | bytes 23724032 | tf_op jit(solution)/vmap(transpose(jvp()))/dot_general | solution.py:9
  193.0 24.2 %fusion.6 = bf16[4096,1792]{1,0:T(8,128)(2,1)S(1)} fusion(f32[4096,1792]{1,0:T(8,128)} %fusion.58, f32[4096,1792]{1,0:T(8,128)} %fusion.60, bf16[4096,1792]{1,0:T(8,128)(2,1)} %convolution_convert_fusion.1), kind=kLoop, calls=%fused_computation.11 | loop fusion | flops 88080384 | bytes 88080384
  217.3 5.2 copy-done
  222.5 14.5 %convolution_convert_fusion.2 = bf16[4096,768]{0,1:T(8,128)(2,1)} fusion(bf16[4096,1792]{1,0:T(8,128)(2,1)S(1)} %fusion.6, bf16[2,768,1792]{2,1,0:T(8,128)(2,1)} %param), kind=kOutput, calls=%fused_computation.61 | convolution fusion | flops 11274289152 | bytes 23724032 | tf_op jit(solution)/vmap(transpose(jvp()))/dot_general | solution.py:20
  237.0 26.6 %fusion.41 = (f32[4096]{0:T(1024)S(1)}, bf16[4096,768]{0,1:T(8,128)(2,1)}) fusion(bf16[1,1,4096,768]{2,3,1,0:T(8,128)(2,1)} %get-tuple-element.10, bf16[4096,768]{0,1:T(8,128)(2,1)} %convolution_convert_fusion.2, bf16[2,768,1792]{2,1,0:T(8,128)(2,1)} %param.3, bf16[4096,1792]{1,0:T(8,128)(2,1)} %convolution_convert_fusion.1, f32[4096,1792]{1,0:T(8,128)} %fusion.58), kind=kOutput, calls=%fused_computation.58 | convolution fusion | flops 11337199616 | bytes 65683456 | tf_op jit(solution)/vmap(transpose(jvp()))/dot_general | solution.py:21
  263.6 8.4 %fusion.48 = bf16[4096,768]{0,1:T(8,128)(2,1)S(1)} fusion(bf16[1,1,4096,768]{2,3,1,0:T(8,128)(2,1)} %get-tuple-element.10, bf16[4096,768]{0,1:T(8,128)(2,1)} %get-tuple-element.12, bf16[1,4096,768]{1,2,0:T(8,128)(2,1)} %copy.1, f32[4096]{0:T(1024)S(1)} %bitcast.368, f32[4096]{0:T(1024)S(1)} %bitcast.371), kind=kLoop, calls=%fused_computation.66 | loop fusion | flops 22020096 | bytes 25198592
  272.0 2.7 copy-done.2
  274.7 17.1 %convolution_bitcast_fusion = f32[1,1792,768]{2,1,0:T(8,128)} fusion(bf16[4096,1792]{1,0:T(8,128)(2,1)} %fusion.26, bf16[4096,768]{0,1:T(8,128)(2,1)S(1)} %fusion.48), kind=kOutput, calls=%fused_computation.81 | convolution fusion | flops 11274289152 | bytes 26476544 | tf_op jit(solution)/vmap(transpose(jvp()))/dot_general | solution.py:9
  291.8 0.1 reduce-scatter.29.cloned.1.call-update
  291.9 0.1 reduce-scatter.23.cloned.1.call-start
  291.9 25.3 %fusion.69 = f32[1,768,1792]{2,1,0:T(8,128)} fusion(bf16[4096,1792]{1,0:T(8,128)(2,1)} %convolution_convert_fusion.1, f32[4096,1792]{1,0:T(8,128)} %fusion.58, bf16[1,1,4096,768]{2,3,1,0:T(8,128)(2,1)} %get-tuple-element.10, f32[4096]{0:T(1024)S(1)} %bitcast.372), kind=kOutput, calls=%fused_computation.79 | convolution fusion | flops 11327766528 | bytes 55853056 | tf_op jit(solution)/vmap(transpose(jvp()))/dot_general | solution.py:21
  317.3 0.1 reduce-scatter.23.cloned.1.call-update
  317.3 0.1 reduce-scatter.25.cloned.1.call-start
  317.4 18.0 %convolution_convert_fusion = bf16[4096,1792]{1,0:T(8,128)(2,1)} fusion(bf16[4096,768]{0,1:T(8,128)(2,1)} %copy-done.2, bf16[2,1792,768]{2,1,0:T(8,128)(2,1)} %param.4), kind=kOutput, calls=%fused_computation.42 | convolution fusion | flops 11281629184 | bytes 23724032 | tf_op jit(solution)/vmap(transpose(jvp()))/dot_general | solution.py:9
  335.4 25.6 %fusion.74 = f32[1,768,1792]{2,1,0:T(8,128)} fusion(bf16[4096,1792]{1,0:T(8,128)(2,1)} %convolution_convert_fusion, f32[4096,1792]{1,0:T(8,128)} %fusion.123, bf16[1,4096,768]{1,2,0:T(8,128)(2,1)} %copy, f32[4096]{0:T(1024)S(1)} %copy-done.10), kind=kOutput, calls=%fused_computation.80 | convolution fusion | flops 11327766528 | bytes 55853056 | tf_op jit(solution)/vmap(transpose(jvp()))/dot_general | solution.py:21
  361.0 0.1 reduce-scatter.25.cloned.1.call-update
  361.1 0.1 reduce-scatter.19.cloned.1.call-start
  361.1 18.4 %fusion.79 = f32[1,768,1792]{2,1,0:T(8,128)} fusion(bf16[4096,1792]{1,0:T(8,128)(2,1)} %copy-done, bf16[1,1,4096,768]{2,3,1,0:T(8,128)(2,1)} %get-tuple-element.10, f32[4096]{0:T(1024)S(1)} %bitcast.373), kind=kOutput, calls=%fused_computation.82 | convolution fusion | flops 11283726336 | bytes 26492928 | tf_op jit(solution)/vmap(transpose(jvp()))/dot_general | solution.py:20
  379.6 0.1 reduce-scatter.19.cloned.1.call-update
  379.6 0.1 reduce-scatter.21.cloned.1.call-start
  379.7 30.6 %fusion.82 = f32[1,768,1792]{2,1,0:T(8,128)} fusion(f32[4096,1792]{1,0:T(8,128)} %fusion.123, f32[4096,1792]{1,0:T(8,128)} %fusion.121, bf16[4096,1792]{1,0:T(8,128)(2,1)} %convolution_convert_fusion, bf16[1,4096,768]{1,2,0:T(8,128)(2,1)} %copy, f32[4096]{0:T(1024)S(1)} %copy-done.10), kind=kOutput, calls=%fused_computation.83 | convolution fusion | flops 11364466688 | bytes 85213184 | tf_op jit(solution)/vmap(transpose(jvp()))/dot_general | solution.py:20
  410.4 0.1 all-gather.14.cloned.1.call-start
  410.5 0.6 dynamic-slice
  411.8 1.4 convert_bitcast_fusion.4
  413.2 1.4 convert_bitcast_fusion.3
  414.6 1.3 fusion.100
  415.9 1.4 convert_bitcast_fusion.6
  417.3 42.5 %reduce-scatter.25.cloned.1.call-done = f32[1,192,1792]{2,1,0:T(8,128)} async-done(((f32[1,768,1792]{2,1,0:T(8,128)}), f32[1,192,1792]{2,1,0:T(8,128)}) %reduce-scatter.25.cloned.1.call-update) | async-done | bytes 1376272
  459.8 1.4 convert_bitcast_fusion.5
  461.2 1.3 fusion.99
  462.5 53.2 %reduce-scatter.19.cloned.1.call-done = f32[1,192,1792]{2,1,0:T(8,128)} async-done(((f32[1,768,1792]{2,1,0:T(8,128)}), f32[1,192,1792]{2,1,0:T(8,128)}) %reduce-scatter.19.cloned.1.call-update) | async-done | bytes 1376272
  515.7 1.4 convert_bitcast_fusion.8
  517.2 54.5 %reduce-scatter.21.cloned.1.call-done = f32[1,192,1792]{2,1,0:T(8,128)} async-done(((f32[1,768,1792]{2,1,0:T(8,128)}), f32[1,192,1792]{2,1,0:T(8,128)}) %reduce-scatter.21.cloned.1.call-update) | async-done | bytes 1376272
  571.7 1.4 convert_bitcast_fusion.7
  573.1 0.8 copy-done.3
  573.9 1.3 fusion.98
  577.2 9.7 %all-reduce.16 = f32[1]{0:T(128)} all-reduce(f32[1]{0:T(128)} %bitcast.50), channel_id=5, replica_groups=mesh['rep'=4,'dp'=4] {'dp'}, use_global_device_ids=true, to_apply=%region_3.4.clone | all-reduce | flops 1 | bytes 8 | tf_op jit(solution)/vmap()/reduce_sum | solution.py:54
  587.6 5.6 fusion.139
  593.3 0.1 all-gather.10.cloned.1.call-start
  593.4 6.0 fusion.141
  599.4 0.1 all-gather.12.cloned.1.call-start
  599.5 5.6 fusion.140
  605.1 42.7 %all-gather.14.cloned.1.call-done = bf16[1,2,1792,768]{3,2,1,0:T(8,128)(2,1)} async-done(((bf16[1,2,448,768]{3,2,1,0:T(8,128)(2,1)}), bf16[1,2,1792,768]{3,2,1,0:T(8,128)(2,1)}) %all-gather.14.cloned.1.call-update) | async-done | bytes 5505040 | tf_op jit(solution)/reshape | solution.py:58
  647.8 57.7 %all-gather.10.cloned.1.call-done = bf16[1,2,768,1792]{3,2,1,0:T(8,128)(2,1)} async-done(((bf16[1,2,192,1792]{3,2,1,0:T(8,128)(2,1)}), bf16[1,2,768,1792]{3,2,1,0:T(8,128)(2,1)}) %all-gather.10.cloned.1.call-update) | async-done | bytes 5505040 | tf_op jit(solution)/reshape | solution.py:58
  705.5 57.7 %all-gather.12.cloned.1.call-done = bf16[1,2,768,1792]{3,2,1,0:T(8,128)(2,1)} async-done(((bf16[1,2,192,1792]{3,2,1,0:T(8,128)(2,1)}), bf16[1,2,768,1792]{3,2,1,0:T(8,128)(2,1)}) %all-gather.12.cloned.1.call-update) | async-done | bytes 5505040 | tf_op jit(solution)/reshape | solution.py:58
  763.2 5.9 copy.5
  769.1 2.8 copy.6
  771.9 0.1 slice-done.2
  772.0 1.1 slice-done.3
  773.1 2.4 copy.7
  (39 shorter events, 0.4 us)
Async XLA Ops:
  7.2 404.6 %reduce-scatter.27.cloned.1.call-start = ((), (), s32[]{:S(2)}) async-start(), calls=%async_computation.13 | async-start | bytes 6881280
  11.3 28.8 %slice-start = ((s8[6291456]{0:T(1024)(128)(4,1)}), s8[2097152]{0:T(1024)(128)(4,1)S(1)}, s32[]{:S(2)}) async-start(s8[6291456]{0:T(1024)(128)(4,1)} %bitcast.359), calls=%async_computation.15 | async-start | bytes 4194304
  20.2 20.0 %copy-start.9 = (f32[4096]{0:T(1024)}, f32[4096]{0:T(1024)S(1)}, u32[]{:S(2)}) copy-start(f32[4096]{0:T(1024)S(1)} %add_rsqrt_fusion) | copy-start | bytes 49156
  20.2 20.0 %slice-start.1 = ((s8[6291456]{0:T(1024)(128)(4,1)}), s8[4194304]{0:T(1024)(128)(4,1)S(1)}, s32[]{:S(2)}) async-start(s8[6291456]{0:T(1024)(128)(4,1)} %bitcast.359), calls=%async_computation.16 | async-start | bytes 8388608
  102.0 0.6 copy-start.5
  102.1 20.9 %copy-start.7 = (f32[1,1,4096]{2,1,0:T(1,128)}, f32[1,1,4096]{2,1,0:T(1,128)S(1)}, u32[]{:S(2)}) copy-start(f32[1,1,4096]{2,1,0:T(1,128)S(1)} %rsqrt.38) | copy-start | bytes 49156
  102.7 20.4 %copy-start.1 = (bf16[1,1,4096,768]{2,3,1,0:T(8,128)(2,1)S(1)}, bf16[1,1,4096,768]{2,3,1,0:T(8,128)(2,1)}, u32[]{:S(2)}) copy-start(bf16[1,1,4096,768]{2,3,1,0:T(8,128)(2,1)} %get-tuple-element.10) | copy-start | bytes 18874372
  166.8 246.4 %reduce-scatter.29.cloned.1.call-start = ((), (), s32[]{:S(2)}) async-start(), calls=%async_computation.14 | async-start | bytes 6881280
  217.3 5.2 copy-start
  237.0 26.6 %copy-start.6 = (f32[4096]{0:T(1024)S(1)}, f32[4096]{0:T(1024)}, u32[]{:S(2)}) copy-start(f32[4096]{0:T(1024)} %copy-done.5) | copy-start | bytes 49156
  237.0 26.6 %copy-start.8 = (f32[1,1,4096]{2,1,0:T(1,128)S(1)}, f32[1,1,4096]{2,1,0:T(1,128)}, u32[]{:S(2)}) copy-start(f32[1,1,4096]{2,1,0:T(1,128)} %copy-done.7) | copy-start | bytes 49156
  272.0 2.7 copy-start.2
  291.9 124.1 %reduce-scatter.23.cloned.1.call-start = ((), (), s32[]{:S(2)}) async-start(), calls=%async_computation.11 | async-start | bytes 6881280
  317.3 18.1 %copy-start.10 = (f32[4096]{0:T(1024)S(1)}, f32[4096]{0:T(1024)}, u32[]{:S(2)}) copy-start(f32[4096]{0:T(1024)} %copy-done.9) | copy-start | bytes 49156
  317.3 142.5 %reduce-scatter.25.cloned.1.call-start = ((), (), s32[]{:S(2)}) async-start(), calls=%async_computation.12 | async-start | bytes 6881280
  361.1 154.7 %reduce-scatter.19.cloned.1.call-start = ((), (), s32[]{:S(2)}) async-start(), calls=%async_computation.9 | async-start | bytes 6881280
  379.6 30.9 %copy-start.11 = (u32[16]{0:T(128)S(1)}, u32[16]{0:T(128)}, u32[]{:S(2)}) copy-start(u32[16]{0:T(128)} %constant.74) | copy-start | bytes 196
  379.6 192.0 %reduce-scatter.21.cloned.1.call-start = ((), (), s32[]{:S(2)}) async-start(), calls=%async_computation.10 | async-start | bytes 6881280
  410.4 237.4 %all-gather.14.cloned.1.call-start = ((), (), s32[]{:S(2)}) async-start(), calls=%async_computation.8 | async-start | bytes 6881280 | tf_op jit(solution)/reshape | solution.py:58
  573.1 0.8 copy-start.3
  593.3 112.2 %all-gather.10.cloned.1.call-start = ((), (), s32[]{:S(2)}) async-start(), calls=%async_computation.6 | async-start | bytes 6881280 | tf_op jit(solution)/reshape | solution.py:58
  599.4 163.9 %all-gather.12.cloned.1.call-start = ((), (), s32[]{:S(2)}) async-start(), calls=%async_computation.7 | async-start | bytes 6881280 | tf_op jit(solution)/reshape | solution.py:58
  763.2 5.9 copy-start.4
  763.2 8.8 %slice-start.2 = ((s8[5505024]{0:T(1024)(128)(4,1)}), s8[4194304]{0:T(1024)(128)(4,1)S(1)}, s32[]{:S(2)}) async-start(s8[5505024]{0:T(1024)(128)(4,1)} %bitcast.361), calls=%async_computation.17 | async-start | bytes 8388608
  769.1 4.0 slice-start.3
Sparse Core Ops, SparseCore 0:
  166.9 56.3 reduce-scatter.26
  292.0 56.3 reduce-scatter.28
  350.7 53.1 reduce-scatter.22
  406.6 53.1 reduce-scatter.24
  462.5 53.1 reduce-scatter.18
  518.5 53.1 reduce-scatter.20
  593.4 54.3 all-gather.13
  650.0 55.5 all-gather.9
  707.7 55.5 all-gather.11
where the time goes:
time: 791 us; the launch traced here: 783 us
  matrix products  314 us (40%)
  waiting for transfers between devices  309 us (39%)
  other arithmetic  91.7 us (12%)
  local copies, waits for them, and re-layouts  39.7 us (5%)
  between operations  17.8 us (2%)
  blocking collectives  9.72 us (1%)
    reshape x3, waiting for transfers between devices, step(): t.reshape(-1, *t.shape[2:])  158 us
    unnamed x15, waiting for transfers between devices  151 us
    dot_general x5, matrix products, layer(): up = jnp.dot(a, w['w_up'], preferred_element_type=jnp.float32)  112 us
    dot_general x5, matrix products, layer(): gate = jnp.dot(a, w['w_gate'], preferred_element_type=jnp.float32)  104 us
    dot_general x5, matrix products, matmul(): jnp.dot(a, w, preferred_element_type=jnp.float32).astype(jnp.bfloat16)  98.7 us
    unnamed x5, other arithmetic  58 us
    unnamed x37, local copies, waits for them, and re-layouts  39.1 us
    reshape x3, other arithmetic, step(): t.reshape(-1, *t.shape[2:])  17.2 us
  transfers between devices with their start and end apart: 9, of which 6 were waited for; matrix products, arithmetic and copies ran while one was open for 33% of the time, Pallas kernels for 0%

commit v1 on v0

v1 whole, which is shorter than its diff:
```python
import functools

import jax
import jax.numpy as jnp
from jax import lax
from jax.experimental import pallas as pl
from jax.experimental.pallas import tpu as pltpu
from jax.sharding import PartitionSpec as P

F32, BF16 = jnp.float32, jnp.bfloat16
VMEM_LIMIT = 66_000_000
CHUNK = 256
MESH = pl.DeviceIdType.MESH
ANY = pl.BlockSpec(memory_space=pl.ANY)


def dot(a, b):
    return jnp.dot(a, b, preferred_element_type=F32)


def dot_t(a, b):
    return lax.dot_general(a, b, (((1,), (1,)), ((), ())), preferred_element_type=F32)


def scale_of(wide):
    return lax.rsqrt(jnp.mean(wide * wide, -1, keepdims=True) + 1e-6)


def whole(shape, at=None):
    if at is None:
        return pl.BlockSpec(shape, lambda *_: (0,) * len(shape), pipeline_mode=pl.Buffered(1))
    return pl.BlockSpec((None, *shape), lambda *_: (at,) + (0,) * len(shape), pipeline_mode=pl.Buffered(1))


def ring():
    n = lax.axis_size("dp")
    me = lax.axis_index("dp")
    return me, (me + 1) % n, (me + n - 1) % n, (me + 2) % n


def meet(others):
    barrier = pltpu.get_barrier_semaphore()
    for other in others:
        pl.semaphore_signal(barrier, inc=1, device_id={"dp": other}, device_id_type=MESH)
    pl.semaphore_wait(barrier, len(others))


def remote(src, dst, send, recv, to):
    return pltpu.make_async_remote_copy(src_ref=src, dst_ref=dst, send_sem=send, recv_sem=recv, device_id={"dp": to}, device_id_type=MESH)


class Scatter:
    def __init__(self, piece, landed, final, send, recv):
        self.piece, self.landed, self.final = piece, landed, final
        self.me, right, left, far = ring()
        self.right, self.left = right, left
        self.routes = (
            lambda: (piece(far, 0), landed.at[0], right),
            lambda: (piece(far, 1), landed.at[1], left),
            lambda: (piece(right, 1), final.at[0, 1], right),
            lambda: (piece(left, 0), final.at[1, 0], left),
            lambda: (landed.at[0], final.at[0, 0], right),
            lambda: (landed.at[1], final.at[1, 1], left),
        )
        self.semaphores = send, recv

    def copy(self, k):
        src, dst, to = self.routes[k]()
        return remote(src, dst, self.semaphores[0].at[k], self.semaphores[1].at[k], to)

    def start(self):
        for k in range(4):
            self.copy(k).start()

    def middle(self):
        for k, own in enumerate((self.piece(self.right, 0), self.piece(self.left, 1))):
            self.copy(k).wait_recv()
            self.landed[k] = (self.landed[k].astype(F32) + own[...].astype(F32)).astype(BF16)
        for k in range(4, 6):
            self.copy(k).start()

    def finish(self, put):
        for k in range(2, 6):
            self.copy(k).wait_recv()
        for half in range(2):
            total = self.piece(self.me, half)[...].astype(F32) + self.final[0, half].astype(F32) + self.final[1, half].astype(F32)
            put(half, total.astype(BF16))
        for k in range(6):
            self.copy(k).wait_send()


def forward_body(x_ref, dy_ref, wg_ref, wu_ref, wd_ref, a_ref, at_ref, h_ref, a2_ref, a2t_ref, dyt_ref, hid):
    x = x_ref[...].astype(F32)
    a = (x * scale_of(x)).astype(BF16)
    a_ref[...] = a
    for j in range(wg_ref.shape[1] // CHUNK):
        at = slice(j * CHUNK, (j + 1) * CHUNK)
        gate, up = dot(a, wg_ref[:, at]), dot(a, wu_ref[:, at])
        hid[:, at] = (gate * jax.nn.sigmoid(gate) * up).astype(BF16)
    at_ref[...] = a.T
    dyt_ref[...] = dy_ref[...].T
    h = (x + dot(hid[...], wd_ref[...]).astype(BF16).astype(F32)).astype(BF16)
    h_ref[...] = h
    wide = h.astype(F32)
    a2 = (wide * scale_of(wide)).astype(BF16)
    a2_ref[...] = a2
    a2t_ref[...] = a2.T


def forward(x, dy, wg, wu, wd, layer, tile=512):
    tokens, d = x.shape
    ff = wg.shape[2]
    rows = pl.BlockSpec((tile, d), lambda i: (i, 0))
    columns = pl.BlockSpec((d, tile), lambda i: (0, i))
    flat, turned = jax.ShapeDtypeStruct((tokens, d), BF16), jax.ShapeDtypeStruct((d, tokens), BF16)
    return pl.pallas_call(
        forward_body,
        grid=(tokens // tile,),
        in_specs=[rows, rows, whole((d, ff), layer), whole((d, ff), layer), whole((ff, d), layer)],
        out_specs=[rows, columns, rows, rows, columns, columns],
        out_shape=[flat, turned, flat, flat, turned, turned],
        scratch_shapes=[pltpu.VMEM((tile, ff), BF16)],
        compiler_params=pltpu.CompilerParams(vmem_limit_bytes=VMEM_LIMIT),
        cost_estimate=pl.CostEstimate(flops=6 * tokens * d * ff, bytes_accessed=16 * tokens * d, transcendentals=tokens * ff),
        name="forward",
    )(x, dy, wg, wu, wd)


def of(n):
    return lambda i: (2 * i) % n


def backward_body(tile, last, a_ref, at_ref, dy_ref, dyt_ref, wg_ref, wu_ref, wd_ref, *rest):
    if last:
        h_ref, dh_ref, dht_ref, gg, gu, gd, pair, down, gw, uw, dw, da, *comm = rest
    else:
        gg_in, gu_in, gd_in, pair_in, down_in, gg, gu, gd, pair, down, gw, uw, dw, *comm = rest
    landed, final, send, recv = comm[:4]
    landed1, final1, landed2, final2, send_d, recv_d = comm[4:10]
    tokens, d = a_ref.shape
    i, chunks = pl.program_id(0), down.shape[0] // CHUNK
    c = of(chunks)(i)
    me, right, left, far = ring()
    wide_rows, tall_rows = gg.shape[1], gd.shape[1]
    layer = 1 if last else 0

    def columns(number):
        return pl.ds(pl.multiple_of(of(chunks)(number) * CHUNK, CHUNK), CHUNK)

    def for_pair(ref, slot):
        def piece(owner, half):
            return ref.at[:, pl.ds(pl.multiple_of(owner * wide_rows + half * (wide_rows // 2), 32), wide_rows // 2), :]

        return Scatter(piece, landed.at[slot], final.at[slot], send.at[slot], recv.at[slot])

    def put_pair(layer, number):
        def put(half, value):
            rows = slice(half * (wide_rows // 2), (half + 1) * (wide_rows // 2))
            gg[layer, rows, columns(number)] = value[0]
            gu[layer, rows, columns(number)] = value[1]

        return put

    def for_down_1():
        def piece(owner, half):
            return down.at[pl.ds(pl.multiple_of(owner * 2 * CHUNK + half * (CHUNK // 2), 32), CHUNK // 2), :]

        return Scatter(piece, landed1, final1, send_d.at[0], recv_d.at[0])

    def put_down_1(half, value):
        gd[layer, pl.ds(pl.multiple_of(me * (2 * CHUNK - tall_rows) + half * (CHUNK // 2), 32), CHUNK // 2), :] = value

    short = 2 * CHUNK - tall_rows

    def start_2(owner, b):
        return b * short + (1 - (owner - b + 3) // 4) * CHUNK

    def for_down_2(ref, slot, b):
        def piece(owner, half):
            return ref.at[pl.ds(pl.multiple_of(owner * tall_rows + start_2(owner, b) + half * (short // 2), 32), short // 2), :]

        return Scatter(piece, landed2.at[slot, b], final2.at[slot, b], send_d.at[1 + 3 * slot + b], recv_d.at[1 + 3 * slot + b])

    def put_down_2(layer, b):
        def put(half, value):
            gd[layer, pl.ds(pl.multiple_of(start_2(me, b) + half * (short // 2), 32), short // 2), :] = value

        return put

    wg, wu, wd = wg_ref[...], wu_ref[...], wd_ref[...]

    def step(t, first):
        rows = pl.ds(t * tile if isinstance(t, int) else pl.multiple_of(t * tile, tile), tile)
        a, dy = a_ref[rows, :], dy_ref[rows, :]
        gate, up, dhid = dot(a, wg), dot(a, wu), dot_t(dy, wd).astype(BF16).astype(F32)
        sig = jax.nn.sigmoid(gate)
        silu = gate * sig
        hid = (silu * up).astype(BF16)
        dup = (dhid * silu).astype(BF16)
        dgate = (dhid * up * (sig + silu * (1 - sig))).astype(BF16)
        at, dyt = at_ref[:, rows], dyt_ref[:, rows]
        for total, term in ((dw, dot(dyt, hid)), (uw, dot(at, dup)), (gw, dot(at, dgate))):
            total[...] = term if first else total[...] + term
        if last:
            da_t = dot_t(dgate, wg) + dot_t(dup, wu)

            @pl.when(i == 0)
            def _():
                da[rows, :] = da_t

            @pl.when(i > 0)
            def _():
                da[rows, :] += da_t

    def steps(start, stop):
        lax.fori_loop(start, stop, lambda t, carry: (step(t, False), carry)[1], 0)

    @pl.when(i == 0)
    def _():
        meet((right, left))
        if not last:
            for_pair(pair_in, chunks).start()
            gg[1] = gg_in[1]
            gu[1] = gu_in[1]
            gd[1] = gd_in[1]

    @pl.when(i > 0)
    def _():
        for_pair(pair, i - 1).start()

    half = tokens // tile // 2
    step(0, True)
    steps(1, half)

    @pl.when(i > 0)
    def _():
        for_pair(pair, i - 1).middle()

    @pl.when(i == 4)
    def _():
        for_down_1().start()

    @pl.when(i == 5)
    def _():
        for_down_1().middle()

    @pl.when(i == 6)
    def _():
        for_down_1().finish(put_down_1)

    if not last:

        @pl.when(i == 0)
        def _():
            for_pair(pair_in, chunks).middle()
            for b in range(3):
                for_down_2(down_in, 0, b).start()

        @pl.when(i == 1)
        def _():
            for b in range(3):
                for_down_2(down_in, 0, b).middle()

        @pl.when(i == 2)
        def _():
            for b in range(3):
                for_down_2(down_in, 0, b).finish(put_down_2(1, b))

    steps(half, 2 * half)

    if not last:

        @pl.when(i == 0)
        def _():
            for_pair(pair_in, chunks).finish(put_pair(1, chunks - 1))

    @pl.when(i > 0)
    def _():
        for_pair(pair, i - 1).finish(put_pair(layer, i - 1))

    pair[0] = gw[...].astype(BF16)
    pair[1] = uw[...].astype(BF16)
    down[pl.ds(pl.multiple_of(c * CHUNK, CHUNK), CHUNK), :] = dw[...].astype(BF16).T

    @pl.when(i == chunks - 1)
    def _():
        if last:

            def finish(h_tile, dh_tile, dht_tile):
                t = pl.program_id(0)
                rows = pl.ds(pl.multiple_of(t * tile, tile), tile)
                wide = h_tile[...].astype(F32)
                scale = scale_of(wide)
                back = da[rows, :].astype(BF16).astype(F32)
                coefficient = jnp.sum(back * wide, -1, keepdims=True) * (scale * scale * scale) * (1.0 / wide.shape[1])
                through = (back * scale - wide * coefficient).astype(BF16)
                dh = (dy_ref[rows, :].astype(F32) + through.astype(F32)).astype(BF16)
                dh_tile[...] = dh
                dht_tile[...] = dh.T

            by_rows = pl.BlockSpec((tile, d), lambda t: (t, 0))
            by_columns = pl.BlockSpec((d, tile), lambda t: (0, t))
            pltpu.emit_pipeline(finish, grid=(tokens // tile,), in_specs=[by_rows], out_specs=[by_rows, by_columns])(h_ref, dh_ref, dht_ref)
        else:
            jobs = [(for_pair(pair, chunks - 1), put_pair(0, chunks - 1))]
            jobs += [(for_down_2(down, 1, b), put_down_2(0, b)) for b in range(3)]
            for job, _ in jobs:
                job.start()
            for job, _ in jobs:
                job.middle()
            for job, put in jobs:
                job.finish(put)


def backward(a, at, dy, dyt, wg, wu, wd, layer, h=None, before=None, group=4, tile=512):
    tokens, d = a.shape
    layers, _, ff = wg.shape
    last = h is not None
    chunks = ff // CHUNK
    flat, turned = whole((tokens, d)), whole((d, tokens))
    by_columns = pl.BlockSpec((None, d, CHUNK), lambda i: (layer, 0, of(chunks)(i)))
    by_rows = pl.BlockSpec((None, CHUNK, d), lambda i: (layer, of(chunks)(i), 0))
    shapes = (layers, d // group, ff), (layers, d // group, ff), (layers, ff // group, d), (2, d, CHUNK), (ff, d)
    out_specs = [whole(s) for s in shapes]
    out_shape = [jax.ShapeDtypeStruct(s, BF16) for s in shapes]
    scratch = [pltpu.VMEM((d, CHUNK), F32)] * 3
    extra, extra_specs = (), []
    if last:
        out_specs = [ANY, ANY] + out_specs
        out_shape = [jax.ShapeDtypeStruct((tokens, d), BF16), jax.ShapeDtypeStruct((d, tokens), BF16)] + out_shape
        scratch += [pltpu.VMEM((tokens, d), F32)]
        extra, extra_specs = (h,), [ANY]
    else:
        extra, extra_specs = before, [whole(s) for s in shapes]
    slots = chunks + 1
    short = 2 * CHUNK - ff // group
    dma = pltpu.SemaphoreType.DMA
    scratch += [
        pltpu.VMEM((slots, 2, 2, d // group // 2, CHUNK), BF16),
        pltpu.VMEM((slots, 2, 2, 2, d // group // 2, CHUNK), BF16),
        dma((slots, 6)),
        dma((slots, 6)),
        pltpu.VMEM((2, CHUNK // 2, d), BF16),
        pltpu.VMEM((2, 2, CHUNK // 2, d), BF16),
        pltpu.VMEM((2, 3, 2, short // 2, d), BF16),
        pltpu.VMEM((2, 3, 2, 2, short // 2, d), BF16),
        dma((7, 6)),
        dma((7, 6)),
    ]
    return pl.pallas_call(
        functools.partial(backward_body, tile, last),
        grid=(chunks,),
        in_specs=[flat, turned, flat, turned, by_columns, by_columns, by_rows] + extra_specs,
        out_specs=out_specs,
        out_shape=out_shape,
        scratch_shapes=scratch,
        compiler_params=pltpu.CompilerParams(vmem_limit_bytes=VMEM_LIMIT, collective_id=1 if last else 2, has_side_effects=True),
        cost_estimate=pl.CostEstimate(flops=(16 if last else 12) * tokens * d * ff, bytes_accessed=16 * tokens * d, transcendentals=tokens * ff),
        name="backward_last" if last else "backward_first",
    )(a, at, dy, dyt, wg, wu, wd, *extra)


def adamw(w, m, v, g):
    m = 0.9 * m + 0.1 * g
    v = 0.95 * v + 0.05 * g * g
    step = m * lax.rsqrt(v + 1e-8) + 0.1 * w
    return (w - 0.02 * step).astype(BF16), m, v


def update_body(count, *refs):
    g, w, m, v, new_w, new_m, new_v = (refs[k : k + 3] for k in range(0, 21, 3))
    held_w, held_m, held_v = (refs[k : k + 3] for k in range(21, 30, 3))
    mine, sums, norm_send, norm_recv, load, store, send, recv = refs[30:]
    me, right, left, far = ring()
    layers = g[0].shape[0]
    loads = {}
    for k in range(3):
        size = g[k].shape[1]
        for layer in range(layers):
            own = w[k].at[layer, pl.ds(pl.multiple_of(me * size, 32), size), :]
            for which, (src, dst) in enumerate(((own, held_w[k].at[layer]), (m[k].at[layer], held_m[k].at[layer]), (v[k].at[layer], held_v[k].at[layer]))):
                loads[k, layer, which] = pltpu.make_async_copy(src, dst, load.at[k, layer, which])
                loads[k, layer, which].start()
    meet((right, left, far))
    total = jnp.float32(0)
    for k in range(3):
        for layer in range(layers):

            def add(r, squares):
                part = g[k][layer, pl.ds(pl.multiple_of(r * 16, 16), 16), :].astype(F32)
                return squares + part * part

            total += jnp.sum(lax.fori_loop(0, g[k].shape[1] // 16, add, jnp.zeros((16, g[k].shape[2]), F32)))
    mine[...] = jnp.full(mine.shape, total, F32)
    sums[me] = mine[...]
    tells = [remote(mine, sums.at[me], norm_send.at[n], norm_recv.at[n], to) for n, to in enumerate((right, left, far))]
    for tell in tells:
        tell.start()
    for tell in tells:
        tell.wait()
    squares = sum(sums[n] for n in range(sums.shape[0]))
    factor = jnp.minimum(1.0, 0.5 * lax.rsqrt(squares / count + 1e-30))[0:1, 0:1]

    copies = []
    for k in range(3):
        size, rows = g[k].shape[1], 32
        half = size // 2
        for layer in range(layers):
            for which in range(3):
                loads[k, layer, which].wait()

            def change(r, carry):
                at = (layer, pl.ds(pl.multiple_of(r * rows, rows), rows), slice(None))
                new = adamw(held_w[k][at].astype(F32), held_m[k][at], held_v[k][at], g[k][at].astype(F32) * factor)
                held_w[k][at], held_m[k][at], held_v[k][at] = new
                return carry

            lax.fori_loop(0, size // rows, change, 0)

            def block(owner, start, length):
                return new_w[k].at[layer, pl.ds(pl.multiple_of(owner * size + start, 32), length), :]

            own, s, r = held_w[k].at[layer], send.at[k, layer], recv.at[k, layer]
            direct = [remote(own, block(me, 0, size), s.at[n], r.at[n], to) for n, to in enumerate((right, left))]
            on = [
                remote(block(left, 0, half), block(left, 0, half), s.at[2], r.at[2], right),
                remote(block(right, half, half), block(right, half, half), s.at[3], r.at[3], left),
            ]
            keep = [pltpu.make_async_copy(own, block(me, 0, size), store.at[k, layer, 0])]
            for which, (held, new) in enumerate(((held_m, new_m), (held_v, new_v))):
                keep.append(pltpu.make_async_copy(held[k].at[layer], new[k].at[layer], store.at[k, layer, 1 + which]))
            for copy in direct + keep:
                copy.start()
            copies.append((direct, on, keep))
    for direct, on, keep in copies:
        for first, second in zip(direct, on, strict=True):
            first.wait_recv()
            second.start()
    for direct, on, keep in copies:
        for copy in on:
            copy.wait()
        for copy in direct:
            copy.wait_send()
        for copy in keep:
            copy.wait()


def update(g, w, m, v):
    count = sum(t.size for t in w)
    layers = w[0].shape[0]
    shapes = [jax.ShapeDtypeStruct(t.shape, t.dtype) for t in (*w, *m, *v)]
    dma = pltpu.SemaphoreType.DMA
    group = w[0].shape[1] // m[0].shape[1]
    vmem = pl.BlockSpec(memory_space=pltpu.VMEM)
    return pl.pallas_call(
        functools.partial(update_body, count),
        in_specs=[vmem] * 3 + [ANY] * 9,
        out_specs=[ANY] * 9,
        out_shape=shapes,
        scratch_shapes=[pltpu.VMEM(t.shape, BF16) for t in m]
        + [pltpu.VMEM(t.shape, F32) for t in (*m, *v)]
        + [pltpu.VMEM((8, 128), F32), pltpu.VMEM((group, 8, 128), F32), dma((3,)), dma((3,))]
        + [dma((3, layers, 3)), dma((3, layers, 3)), dma((3, layers, 4)), dma((3, layers, 4))],
        compiler_params=pltpu.CompilerParams(vmem_limit_bytes=VMEM_LIMIT, collective_id=3, has_side_effects=True),
        name="update",
    )(*g, *w, *m, *v)


def solution(mesh):
    group = mesh.shape["dp"]

    def step(x, dy, *arrays):
        w, m, v = (arrays[i : i + 3] for i in (0, 3, 6))
        x, dy = x[0], dy[0]
        a1, a1t, h1, a2, a2t, dyt = forward(x, dy, *w, 0)
        dh, dht, *before = backward(a2, a2t, dy, dyt, *w, 1, h=h1, group=group)
        gg, gu, gd, *_ = backward(a1, a1t, dh, dht, *w, 0, before=before, group=group)
        return tuple(update((gg, gu, gd), w, m, v))

    sequence, rows = P(("rep", "dp"), None, None), P(None, "dp", None)
    return jax.shard_map(
        step,
        mesh=mesh,
        in_specs=(sequence,) * 2 + (P(),) * 3 + (rows,) * 6,
        out_specs=(P("rep", None, None),) * 3 + (P("rep", "dp", None),) * 6,
        check_vma=False,
    )
```

time: 791 us -> 493 us (0.62); the launches traced: 783 us -> 492 us
  Pallas kernels: 0 us -> 463 us
  matrix products: 314 us -> 0 us
  waiting for transfers between devices: 309 us -> 0 us
  other arithmetic: 91.7 us -> 0.01 us
  between operations: 17.8 us -> 0.69 us
  local copies, waits for them, and re-layouts: 39.7 us -> 29 us
  blocking collectives: 9.72 us -> 0 us
    pallas_call x0 -> x4, Pallas kernels: none -> 463 us  [the longest x2 274 us: backward(): pl.pallas_call(functools.partial(backward_body, tile, last), grid=(chunks...]
    dot_general x15 -> x0, matrix products: 314 us -> none  [the longest x5 112 us: layer(): up = jnp.dot(a, w['w_up'], preferred_element_type=jnp.float32)]
    reshape x3 -> x0, waiting for transfers between devices: 158 us -> none  [step(): t.reshape(-1, *t.shape[2:])]
    unnamed x15 -> x0, waiting for transfers between devices: 151 us -> none
    unnamed x5 -> x1, other arithmetic: 58 us -> 0.01 us
    reshape x3 -> x0, other arithmetic: 17.2 us -> none  [step(): t.reshape(-1, *t.shape[2:])]
    unnamed x37 -> x27, local copies, waits for them, and re-layouts: 39.1 us -> 29 us
    reduce_sum x1 -> x0, blocking collectives: 9.72 us -> none  [of_a_group(): jnp.sum(g * g)]
  transfers between devices with their start and end apart: 9 -> 0, of which waited for: 6 -> 0; matrix products, arithmetic and copies ran while one was open for 33% -> 0% of each run, Pallas kernels for 0% -> 0%
where the time goes in v1:
time: 493 us; the launch traced here: 492 us
  Pallas kernels  463 us (94%)
  local copies, waits for them, and re-layouts  29 us (6%)
    pallas_call x2, Pallas kernels, backward(): pl.pallas_call(functools.partial(backward_body, tile, last), grid=(chunks...  274 us
    pallas_call x1, Pallas kernels, update(): pl.pallas_call(functools.partial(update_body, count), in_specs=[vmem] * 3...  142 us
    pallas_call x1, Pallas kernels, forward(): pl.pallas_call(forward_body, grid=(tokens // tile,), in_specs=[rows, rows...  46.9 us
    unnamed x27, local copies, waits for them, and re-layouts  29 us

profile of v1, /device:TPU:112, one launch (start us, length us, event | category | flops | bytes accessed | tf_op | source)
XLA Modules:
  0.0 492.5 jit_solution(9049325636958716166)
XLA Ops:
  0.6 46.9 %forward.1 = (bf16[4096,768]{1,0:T(8,128)(2,1)}, bf16[768,4096]{1,0:T(8,128)(2,1)}, bf16[4096,768]{1,0:T(8,128)(2,1)}, bf16[4096,768]{1,0:T(8,128)(2,1)}, bf16[7...) custom-call(bf16[4096,768]{1,0:T(8,128)(2,1)} %bitcast.4, bf16[4096,768]{1,0:T(8,128)(2,1)} %bitcast.5, ...), custom_call_target="tpu_custom_call" | custom-call | flops 33822867456 | bytes 50331648 | tf_op jit(solution)/shard_map/forward/pallas_call | solution.py:116
  47.5 147.4 %backward_last.1 = (bf16[4096,768]{1,0:T(8,128)(2,1)}, bf16[768,4096]{1,0:T(8,128)(2,1)}, bf16[2,192,1792]{2,1,0:T(8,128)(2,1)}, bf16[2,192,1792]{2,1,0:T(8,128)...) custom-call(bf16[4096,768]{1,0:T(8,128)(2,1)} %get-tuple-element.27.a_ref, ...), custom_call_target="tpu_custom_call" | custom-call | flops 90194313216 | bytes 50331648 | tf_op jit(solution)/shard_map/backward_last/pallas_call | solution.py:350
  194.9 126.2 %backward_first.1 = (bf16[2,192,1792]{2,1,0:T(8,128)(2,1)}, bf16[2,192,1792]{2,1,0:T(8,128)(2,1)}, bf16[2,448,768]{2,1,0:T(8,128)(2,1)}, bf16[2,768,256]{2,1,0:T(8,128)(2,1)}, bf16[1792,768]{1,0:T(8,128)(2,1)}) custom-call(bf16[4096,768]{1,0:T(8,128)(2,1)} %get-tuple-element.25.a_ref, bf16[768,4096]{1,0:T(8,128)(2,1)} %get-tuple-element.26.at_ref, ...), custom_call_target="tpu_custom_call" | custom-call | flops 67645734912 | bytes 50331648 | tf_op jit(solution)/shard_map/backward_first/pallas_call | solution.py:350
  321.1 142.3 %update.1 = (bf16[2,768,1792]{2,1,0:T(8,128)(2,1)}, bf16[2,768,1792]{2,1,0:T(8,128)(2,1)}, bf16[2,1792,768]{2,1,0:T(8,128)(2,1)}, f32[2,192,1792]{2,1,0:T(8,128)...) custom-call(bf16[2,192,1792]{2,1,0:T(8,128)(2,1)} %get-tuple-element, ...), custom_call_target="tpu_custom_call" | custom-call | tf_op jit(solution)/shard_map/update/pallas_call | solution.py:455
  463.4 0.0 copy-start
  463.4 0.0 slice-start
  463.4 5.9 %copy.29 = bf16[2,768,1792]{2,1,0:T(8,128)(2,1)} copy(bf16[2,768,1792]{2,1,0:T(8,128)(2,1)} %get-tuple-element.50) | data formatting | bytes 11010048
  469.3 0.0 copy-done
  469.3 0.0 slice-start.1
  469.3 2.8 copy.30
  472.1 0.1 slice-done
  472.2 1.1 slice-done.1
  473.3 0.0 copy-start.6
  473.3 2.8 copy.31
  476.1 1.0 copy-done.6
  477.1 0.0 copy-start.5
  477.1 1.5 copy.32
  478.6 1.2 copy-done.5
  479.8 0.0 copy-start.4
  479.8 1.5 copy.33
  481.4 1.2 copy-done.4
  482.6 0.0 copy-start.3
  482.6 1.5 copy.34
  484.1 1.2 copy-done.3
  485.4 0.0 copy-start.2
  485.4 1.5 copy.35
  486.9 1.2 copy-done.2
  488.2 0.0 copy-start.1
  488.2 1.5 copy.36
  489.7 1.2 copy-done.1
  490.9 1.5 copy.37
  (1 shorter events, 0.0 us)
Async XLA Ops:
  463.4 5.9 %copy-start = (bf16[2,768,1792]{2,1,0:T(8,128)(2,1)S(1)}, bf16[2,768,1792]{2,1,0:T(8,128)(2,1)}, u32[]{:S(2)}) copy-start(bf16[2,768,1792]{2,1,0:T(8,128)(2,1)} %get-tuple-element.51) | copy-start | bytes 16515076
  463.4 8.7 %slice-start = ((s8[5505024]{0:T(1024)(128)(4,1)}), s8[4194304]{0:T(1024)(128)(4,1)S(1)}, s32[]{:S(2)}) async-start(s8[5505024]{0:T(1024)(128)(4,1)} %bitcast.2), calls=%async_computation | async-start | bytes 8388608
  469.3 4.0 slice-start.1
  473.3 3.8 copy-start.6
  477.1 2.8 copy-start.5
  479.8 2.8 copy-start.4
  482.6 2.8 copy-start.3
  485.4 2.8 copy-start.2
  488.2 2.8 copy-start.1

commit v2 on v1

v2 whole, which is shorter than its diff:
```python
import functools

import jax
import jax.numpy as jnp
from jax import lax
from jax.experimental import pallas as pl
from jax.experimental.pallas import tpu as pltpu
from jax.sharding import PartitionSpec as P

F32, BF16 = jnp.float32, jnp.bfloat16
VMEM_LIMIT = 66_000_000
CHUNK = 256
MESH = pl.DeviceIdType.MESH
ANY = pl.BlockSpec(memory_space=pl.ANY)


def dot(a, b):
    return jnp.dot(a, b, preferred_element_type=F32)


def dot_t(a, b):
    return lax.dot_general(a, b, (((1,), (1,)), ((), ())), preferred_element_type=F32)


def scale_of(wide):
    return lax.rsqrt(jnp.mean(wide * wide, -1, keepdims=True) + 1e-6)


def whole(shape, at=None):
    if at is None:
        return pl.BlockSpec(shape, lambda *_: (0,) * len(shape), pipeline_mode=pl.Buffered(1))
    return pl.BlockSpec((None, *shape), lambda *_: (at,) + (0,) * len(shape), pipeline_mode=pl.Buffered(1))


def ring():
    n = lax.axis_size("dp")
    me = lax.axis_index("dp")
    return me, (me + 1) % n, (me + n - 1) % n, (me + 2) % n


def meet(others):
    barrier = pltpu.get_barrier_semaphore()
    for other in others:
        pl.semaphore_signal(barrier, inc=1, device_id={"dp": other}, device_id_type=MESH)
    pl.semaphore_wait(barrier, len(others))


def remote(src, dst, send, recv, to):
    return pltpu.make_async_remote_copy(src_ref=src, dst_ref=dst, send_sem=send, recv_sem=recv, device_id={"dp": to}, device_id_type=MESH)


class Scatter:
    def __init__(self, piece, landed, final, send, recv):
        self.piece, self.landed, self.final = piece, landed, final
        self.me, right, left, far = ring()
        self.right, self.left = right, left
        self.routes = (
            lambda: (piece(far, 0), landed.at[0], right),
            lambda: (piece(far, 1), landed.at[1], left),
            lambda: (piece(right, 1), final.at[0, 1], right),
            lambda: (piece(left, 0), final.at[1, 0], left),
            lambda: (landed.at[0], final.at[0, 0], right),
            lambda: (landed.at[1], final.at[1, 1], left),
        )
        self.semaphores = send, recv

    def copy(self, k):
        src, dst, to = self.routes[k]()
        return remote(src, dst, self.semaphores[0].at[k], self.semaphores[1].at[k], to)

    def start(self):
        for k in range(4):
            self.copy(k).start()

    def middle(self):
        for k, own in enumerate((self.piece(self.right, 0), self.piece(self.left, 1))):
            self.copy(k).wait_recv()
            self.landed[k] = (self.landed[k].astype(F32) + own[...].astype(F32)).astype(BF16)
        for k in range(4, 6):
            self.copy(k).start()

    def finish(self, put):
        for k in range(2, 6):
            self.copy(k).wait_recv()
        for half in range(2):
            total = self.piece(self.me, half)[...].astype(F32) + self.final[0, half].astype(F32) + self.final[1, half].astype(F32)
            put(half, total.astype(BF16))
        for k in range(6):
            self.copy(k).wait_send()


def forward_body(x_ref, dy_ref, wg_ref, wu_ref, wd_ref, gate_ref, up_ref, at_ref, h_ref, a2_ref, a2t_ref, dyt_ref, hid):
    x = x_ref[...].astype(F32)
    a = (x * scale_of(x)).astype(BF16)
    for j in range(wg_ref.shape[1] // CHUNK):
        at = slice(j * CHUNK, (j + 1) * CHUNK)
        gate, up = dot(a, wg_ref[:, at]), dot(a, wu_ref[:, at])
        gate_ref[j], up_ref[j] = gate, up
        hid[:, at] = (gate * jax.nn.sigmoid(gate) * up).astype(BF16)
    at_ref[...] = a.T
    dyt_ref[...] = dy_ref[...].T
    h = (x + dot(hid[...], wd_ref[...]).astype(BF16).astype(F32)).astype(BF16)
    h_ref[...] = h
    wide = h.astype(F32)
    a2 = (wide * scale_of(wide)).astype(BF16)
    a2_ref[...] = a2
    a2t_ref[...] = a2.T


def forward(x, dy, wg, wu, wd, layer, tile=512):
    tokens, d = x.shape
    ff = wg.shape[2]
    chunks = ff // CHUNK
    rows = pl.BlockSpec((tile, d), lambda i: (i, 0))
    columns = pl.BlockSpec((d, tile), lambda i: (0, i))
    kept = pl.BlockSpec((chunks, tile, CHUNK), lambda i: (0, i, 0))
    flat, turned = jax.ShapeDtypeStruct((tokens, d), BF16), jax.ShapeDtypeStruct((d, tokens), BF16)
    by_chunk = jax.ShapeDtypeStruct((chunks, tokens, CHUNK), F32)
    return pl.pallas_call(
        forward_body,
        grid=(tokens // tile,),
        in_specs=[rows, rows, whole((d, ff), layer), whole((d, ff), layer), whole((ff, d), layer)],
        out_specs=[kept, kept, columns, rows, rows, columns, columns],
        out_shape=[by_chunk, by_chunk, turned, flat, flat, turned, turned],
        scratch_shapes=[pltpu.VMEM((tile, ff), BF16)],
        compiler_params=pltpu.CompilerParams(vmem_limit_bytes=VMEM_LIMIT),
        cost_estimate=pl.CostEstimate(flops=6 * tokens * d * ff, bytes_accessed=16 * tokens * d, transcendentals=tokens * ff),
        name="forward",
    )(x, dy, wg, wu, wd)


def of(n):
    return lambda i: (2 * i) % n


def backward_body(tile, unroll, last, *refs):
    if last:
        a_in, at_in, dy_in, dyt_in, wg_ref, wu_ref, wd_ref, h_ref, dh_ref, dht_ref, gg, gu, gd, pair, down, a_ref, *rest = refs
    else:
        gate_ref, up_ref, at_in, dy_in, dyt_in, wd_ref, gg_in, gu_in, gd_in, pair_in, down_in, gg, gu, gd, pair, down, *rest = refs
    at_ref, dy_ref, dyt_ref, loads, gw, uw, dw, landed, final, send, recv, landed1, final1, send_d, recv_d, *rest = rest
    if last:
        da, h, h_sem, out_sem = rest
    else:
        landed2, final2 = rest
    tokens, d = dy_ref.shape
    i, chunks = pl.program_id(0), down.shape[0] // CHUNK
    c = of(chunks)(i)
    me, right, left, far = ring()
    wide_rows, tall_rows = gg.shape[-2], gd.shape[-2]
    layer = () if last else (0,)

    def columns(number):
        return pl.ds(pl.multiple_of(of(chunks)(number) * CHUNK, CHUNK), CHUNK)

    def for_pair(ref, slot):
        def piece(owner, half):
            return ref.at[:, pl.ds(pl.multiple_of(owner * wide_rows + half * (wide_rows // 2), 32), wide_rows // 2), :]

        return Scatter(piece, landed.at[slot], final.at[slot], send.at[slot], recv.at[slot])

    def put_pair(layer, number):
        def put(half, value):
            rows = slice(half * (wide_rows // 2), (half + 1) * (wide_rows // 2))
            gg[(*layer, rows, columns(number))] = value[0]
            gu[(*layer, rows, columns(number))] = value[1]

        return put

    def for_down_1():
        def piece(owner, half):
            return down.at[pl.ds(pl.multiple_of(owner * 2 * CHUNK + half * (CHUNK // 2), 32), CHUNK // 2), :]

        return Scatter(piece, landed1, final1, send_d.at[0], recv_d.at[0])

    def put_down_1(half, value):
        gd[(*layer, pl.ds(pl.multiple_of(me * (2 * CHUNK - tall_rows) + half * (CHUNK // 2), 32), CHUNK // 2), slice(None))] = value

    short = 2 * CHUNK - tall_rows

    def start_2(owner, b):
        return b * short + (1 - (owner - b + 3) // 4) * CHUNK

    def for_down_2(ref, slot, b):
        def piece(owner, half):
            return ref.at[pl.ds(pl.multiple_of(owner * tall_rows + start_2(owner, b) + half * (short // 2), 32), short // 2), :]

        return Scatter(piece, landed2.at[slot, b], final2.at[slot, b], send_d.at[1 + 3 * slot + b], recv_d.at[1 + 3 * slot + b])

    def put_down_2(at, b):
        def put(half, value):
            gd[at, pl.ds(pl.multiple_of(start_2(me, b) + half * (short // 2), 32), short // 2), :] = value

        return put

    wd = wd_ref[...]
    if last:
        wg, wu = wg_ref[...], wu_ref[...]

    def rows_of(t):
        return pl.ds(pl.multiple_of(t * tile, tile), tile)

    def load(t):
        by_rows, by_columns = (rows_of(t), slice(None)), (slice(None), rows_of(t))
        arrays = [(dy_in, dy_ref, by_rows), (at_in, at_ref, by_columns), (dyt_in, dyt_ref, by_columns)]
        if last:
            arrays.append((a_in, a_ref, by_rows))
        return [pltpu.make_async_copy(src.at[at], dst.at[at], loads.at[k, t]) for k, (src, dst, at) in enumerate(arrays)]

    def fetch(t, slot):
        return pltpu.make_async_copy(h_ref.at[rows_of(t), :], h.at[slot], h_sem.at[slot])

    def hand_on(t):
        by_rows, by_columns = (rows_of(t), slice(None)), (slice(None), rows_of(t))
        return [
            pltpu.make_async_copy(dy_ref.at[by_rows], dh_ref.at[by_rows], out_sem.at[0, t]),
            pltpu.make_async_copy(dyt_ref.at[by_columns], dht_ref.at[by_columns], out_sem.at[1, t]),
        ]

    def step(t, ends=False):
        rows = rows_of(t)
        if last:
            a = a_ref[rows, :]
            gate, up = dot(a, wg), dot(a, wu)
        else:
            gate, up = gate_ref[rows, :], up_ref[rows, :]
        dy = dy_ref[rows, :]
        dhid = dot_t(dy, wd).astype(BF16).astype(F32)
        sig = jax.nn.sigmoid(gate)
        silu = gate * sig
        hid = (silu * up).astype(BF16)
        dup = (dhid * silu).astype(BF16)
        dgate = (dhid * up * (sig + silu * (1 - sig))).astype(BF16)
        at, dyt = at_ref[:, rows], dyt_ref[:, rows]
        dw[...] += dot(dyt, hid)
        uw[...] += dot(at, dup)
        gw[...] += dot(at, dgate)
        if last:
            da_t = dot_t(dgate, wg) + dot_t(dup, wu)
            if not ends:
                da[rows, :] = jnp.where(i == 0, da_t, da[rows, :] + da_t)
            else:
                wide = h[t % 2].astype(F32)
                scale = scale_of(wide)
                back = (da[rows, :] + da_t).astype(BF16).astype(F32)
                coefficient = jnp.sum(back * wide, -1, keepdims=True) * (scale * scale * scale) * (1.0 / wide.shape[1])
                through = (back * scale - wide * coefficient).astype(BF16)
                dh = (dy.astype(F32) + through.astype(F32)).astype(BF16)
                dy_ref[rows, :] = dh
                dyt_ref[:, rows] = dh.T

    def steps(start, stop):
        def some(n, carry):
            @pl.when(i == 0)
            def _():
                for k in range(unroll):
                    for copy in load(n * unroll + k):
                        copy.wait()

            for k in range(unroll):
                step(n * unroll + k)
            return carry

        def some_last(t, carry):
            fetch(t, t % 2).wait()

            @pl.when(t + 1 < tokens // tile)
            def _():
                fetch(t + 1, (t + 1) % 2).start()

            @pl.when(t > 0)
            def _():
                for copy in hand_on(t - 1):
                    copy.start()

            step(t, ends=True)
            return carry

        if last:

            @pl.when(i < chunks - 1)
            def _():
                lax.fori_loop(start // unroll, stop // unroll, some, 0)

            @pl.when(i == chunks - 1)
            def _():
                if start == 0:
                    fetch(0, 0).start()
                lax.fori_loop(start, stop, some_last, 0)

        else:
            lax.fori_loop(start // unroll, stop // unroll, some, 0)

    for total in (gw, uw, dw):
        total[...] = jnp.zeros_like(total)

    def own(number):
        return for_pair(pair if last else pair.at[number % 3], number)

    @pl.when(i == 0)
    def _():
        for t in range(tokens // tile):
            for copy in load(t):
                copy.start()
        meet((right, left))
        if not last:
            for_pair(pair_in, chunks).start()
            for b in range(3):
                for_down_2(down_in, 0, b).start()
            gg[1] = gg_in[...]
            gu[1] = gu_in[...]
            gd[1] = gd_in[...]

    @pl.when(i > 0)
    def _():
        own(i - 1).start()

    if last:
        half = tokens // tile // 2
        steps(0, half)

        @pl.when(i > 0)
        def _():
            own(i - 1).middle()

    @pl.when(i == 4)
    def _():
        for_down_1().start()

    if not last:

        @pl.when(i == 1)
        def _():
            for_pair(pair_in, chunks).middle()

        @pl.when(i > 1)
        def _():
            own(i - 2).middle()

        @pl.when(i == 2)
        def _():
            for_pair(pair_in, chunks).finish(put_pair((1,), chunks - 1))
            for b in range(3):
                for_down_2(down_in, 0, b).middle()

        @pl.when(i > 2)
        def _():
            own(i - 3).finish(put_pair(layer, i - 3))

        @pl.when(i == 4)
        def _():
            for b in range(3):
                for_down_2(down_in, 0, b).finish(put_down_2(1, b))

    @pl.when(i == (5 if last else 6))
    def _():
        for_down_1().middle()

    if last:

        @pl.when(i == 6)
        def _():
            for_down_1().finish(put_down_1)

        steps(half, 2 * half)

        @pl.when(i > 0)
        def _():
            own(i - 1).finish(put_pair(layer, i - 1))

    else:
        steps(0, tokens // tile)

    at = () if last else (i % 3,)
    pair[(*at, 0)] = gw[...].astype(BF16)
    pair[(*at, 1)] = uw[...].astype(BF16)
    down[pl.ds(pl.multiple_of(c * CHUNK, CHUNK), CHUNK), :] = dw[...].astype(BF16).T

    @pl.when(i == chunks - 1)
    def _():
        if last:
            for copy in hand_on(tokens // tile - 1):
                copy.start()
            for t in range(tokens // tile):
                for copy in hand_on(t):
                    copy.wait()
        else:
            rest = [(for_down_2(down, 1, b), put_down_2(0, b)) for b in range(3)]
            jobs = [own(chunks - 3 + n) for n in range(3)]
            for job in (jobs[2], *(job for job, _ in rest)):
                job.start()
            jobs[1].middle()
            jobs[0].finish(put_pair(layer, chunks - 3))
            for job in (jobs[2], *(job for job, _ in rest)):
                job.middle()
            jobs[1].finish(put_pair(layer, chunks - 2))
            for_down_1().finish(put_down_1)
            for job, put in ((jobs[2], put_pair(layer, chunks - 1)), *rest):
                job.finish(put)


def backward(source, at, dy, dyt, w, layer, h=None, before=None, group=4, tile=512, unroll=1):
    tokens, d = dy.shape
    layers, _, ff = w[0].shape
    last = h is not None
    chunks = ff // CHUNK
    by_columns = pl.BlockSpec((None, d, CHUNK), lambda i: (layer, 0, of(chunks)(i)))
    by_rows = pl.BlockSpec((None, CHUNK, d), lambda i: (layer, of(chunks)(i), 0))
    shapes = [(d // group, ff), (d // group, ff), (ff // group, d), (2, d, CHUNK), (ff, d)]
    dma = pltpu.SemaphoreType.DMA
    slots = chunks - 1 if last else chunks + 1
    part, short = d // group // 2, 2 * CHUNK - ff // group
    scratch = [pltpu.VMEM((d, tokens), BF16), pltpu.VMEM((tokens, d), BF16), pltpu.VMEM((d, tokens), BF16), dma((4, tokens // tile))]
    scratch += [pltpu.VMEM((d, CHUNK), F32)] * 3
    scratch += [pltpu.VMEM((slots, 2, 2, part, CHUNK), BF16), pltpu.VMEM((slots, 2, 2, 2, part, CHUNK), BF16), dma((slots, 6)), dma((slots, 6))]
    scratch += [pltpu.VMEM((2, CHUNK // 2, d), BF16), pltpu.VMEM((2, 2, CHUNK // 2, d), BF16), dma((7, 6)), dma((7, 6))]
    if last:
        out_shape = [jax.ShapeDtypeStruct(s, BF16) for s in ((tokens, d), (d, tokens), *shapes)]
        out_specs = [ANY, ANY] + [whole(s) for s in shapes]
        args = (source, at, dy, dyt, *w, h)
        in_specs = [ANY] * 4 + [by_columns, by_columns, by_rows, ANY]
        scratch = [pltpu.VMEM((tokens, d), BF16)] + scratch + [pltpu.VMEM((tokens, d), F32)]
        scratch += [pltpu.VMEM((2, tile, d), BF16), dma((2,)), dma((2, tokens // tile))]
    else:
        by_chunk = pl.BlockSpec((None, tokens, CHUNK), lambda i: (of(chunks)(i), 0, 0))
        args = (*source, at, dy, dyt, w[2], *before)
        in_specs = [by_chunk, by_chunk] + [ANY] * 3 + [by_rows] + [whole(s) for s in shapes]
        shapes = [(layers, *s) for s in shapes[:3]]
        out_shape = [jax.ShapeDtypeStruct(s, BF16) for s in shapes]
        out_specs = [whole(s) for s in shapes]
        scratch = [pltpu.VMEM((3, 2, d, CHUNK), BF16), pltpu.VMEM((ff, d), BF16)] + scratch
        scratch += [pltpu.VMEM((2, 3, 2, short // 2, d), BF16), pltpu.VMEM((2, 3, 2, 2, short // 2, d), BF16)]
    return pl.pallas_call(
        functools.partial(backward_body, tile, unroll, last),
        grid=(chunks,),
        in_specs=in_specs,
        out_specs=out_specs,
        out_shape=out_shape,
        scratch_shapes=scratch,
        compiler_params=pltpu.CompilerParams(vmem_limit_bytes=VMEM_LIMIT, collective_id=1 if last else 2, has_side_effects=True),
        cost_estimate=pl.CostEstimate(flops=(16 if last else 8) * tokens * d * ff, bytes_accessed=16 * tokens * d, transcendentals=tokens * ff),
        name="backward_last" if last else "backward_first",
    )(*args)


def adamw(w, m, v, g):
    m = 0.9 * m + 0.1 * g
    v = 0.95 * v + 0.05 * g * g
    step = m * lax.rsqrt(v + 1e-8) + 0.1 * w
    return (w - 0.02 * step).astype(BF16), m, v


def update_body(count, *refs):
    g_in, w, m, v, new_w, new_m, new_v, g = (refs[k : k + 3] for k in range(0, 24, 3))
    mine, sums, norm_send, norm_recv, load, send, recv = refs[24:]
    me, right, left, far = ring()
    layers = g[0].shape[0]
    loads = {}

    def fetch(which, k, layer, src, dst, at):
        loads[k, layer, which] = pltpu.make_async_copy(src[k].at[at], dst[k].at[at], load.at[k, layer, which])
        loads[k, layer, which].start()

    parts = [(k, layer) for k in range(3) for layer in range(layers)]
    for k, layer in parts:
        fetch(3, k, layer, g_in, g, layer)
    for k, layer in parts:
        fetch(0, k, layer, w, new_w, (layer, pl.ds(pl.multiple_of(me * g[k].shape[1], 32), g[k].shape[1])))
        fetch(1, k, layer, m, new_m, layer)
        fetch(2, k, layer, v, new_v, layer)
    meet((right, left, far))
    total = jnp.float32(0)
    for k in range(3):
        for layer in range(layers):
            loads[k, layer, 3].wait()

            def add(r, squares):
                part = g[k][layer, pl.ds(pl.multiple_of(r * 16, 16), 16), :].astype(F32)
                return squares + part * part

            total += jnp.sum(lax.fori_loop(0, g[k].shape[1] // 16, add, jnp.zeros((16, g[k].shape[2]), F32)))
    mine[...] = jnp.full(mine.shape, total, F32)
    sums[me] = mine[...]
    tells = [remote(mine, sums.at[me], norm_send.at[n], norm_recv.at[n], to) for n, to in enumerate((right, left, far))]
    for tell in tells:
        tell.start()
    for tell in tells:
        tell.wait()
    squares = sum(sums[n] for n in range(sums.shape[0]))
    factor = jnp.minimum(1.0, 0.5 * lax.rsqrt(squares / count + 1e-30))[0:1, 0:1]

    copies = []
    for k in range(3):
        size, rows = g[k].shape[1], 32
        half = size // 2
        for layer in range(layers):
            for which in range(3):
                loads[k, layer, which].wait()

            def change(r, carry):
                at = (layer, pl.ds(pl.multiple_of(r * rows, rows), rows), slice(None))
                own = (layer, pl.ds(pl.multiple_of(me * size + r * rows, rows), rows), slice(None))
                new = adamw(new_w[k][own].astype(F32), new_m[k][at], new_v[k][at], g[k][at].astype(F32) * factor)
                new_w[k][own], new_m[k][at], new_v[k][at] = new
                return carry

            lax.fori_loop(0, size // rows, change, 0)

            def block(owner, start, length):
                return new_w[k].at[layer, pl.ds(pl.multiple_of(owner * size + start, 32), length), :]

            s, r = send.at[k, layer], recv.at[k, layer]
            direct = [remote(block(me, 0, size), block(me, 0, size), s.at[n], r.at[n], to) for n, to in enumerate((right, left))]
            on = [
                remote(block(left, 0, half), block(left, 0, half), s.at[2], r.at[2], right),
                remote(block(right, half, half), block(right, half, half), s.at[3], r.at[3], left),
            ]
            for copy in direct:
                copy.start()
            copies.append((direct, on))
    for direct, on in copies:
        for first, second in zip(direct, on, strict=True):
            first.wait_recv()
            second.start()
    for direct, on in copies:
        for copy in on:
            copy.wait()
        for copy in direct:
            copy.wait_send()


def update(g, w, m, v):
    count = sum(t.size for t in w)
    layers = w[0].shape[0]
    shapes = [pltpu.VMEM(t.shape, t.dtype) for t in (*w, *m, *v)]
    dma = pltpu.SemaphoreType.DMA
    group = w[0].shape[1] // m[0].shape[1]
    vmem = pl.BlockSpec(memory_space=pltpu.VMEM)
    return pl.pallas_call(
        functools.partial(update_body, count),
        in_specs=[ANY] * 12,
        out_specs=[vmem] * 9,
        out_shape=shapes,
        scratch_shapes=[pltpu.VMEM(t.shape, BF16) for t in m]
        + [pltpu.VMEM((8, 128), F32), pltpu.VMEM((group, 8, 128), F32), dma((3,)), dma((3,))]
        + [dma((3, layers, 4)), dma((3, layers, 4)), dma((3, layers, 4))],
        compiler_params=pltpu.CompilerParams(vmem_limit_bytes=28_000_000, collective_id=3, has_side_effects=True),
        name="update",
    )(*g, *w, *m, *v)


def solution(mesh):
    group = mesh.shape["dp"]

    def step(x, dy, *arrays):
        w, m, v = (arrays[i : i + 3] for i in (0, 3, 6))
        x, dy = x[0], dy[0]
        gate, up, a1t, h1, a2, a2t, dyt = forward(x, dy, *w, 0)
        dh, dht, *before = backward(a2, a2t, dy, dyt, w, 1, h=h1, group=group)
        g = backward((gate, up), a1t, dh, dht, w, 0, before=before, group=group, unroll=4)
        return tuple(update(g, w, m, v))

    sequence, rows = P(("rep", "dp"), None, None), P(None, "dp", None)
    return jax.shard_map(
        step,
        mesh=mesh,
        in_specs=(sequence,) * 2 + (P(),) * 3 + (rows,) * 6,
        out_specs=(P("rep", None, None),) * 3 + (P("rep", "dp", None),) * 6,
        check_vma=False,
    )
```

time: 493 us -> 446 us (0.905)
  Pallas kernels: 463 us -> 428 us
  local copies, waits for them, and re-layouts: 29 us -> 16.5 us
    pallas_call x3, Pallas kernels: 416 us -> 379 us  [the longest x2 236 us: backward(): pl.pallas_call(functools.partial(backward_body, tile, unroll, last), grid...]
    unnamed x27 -> x9, local copies, waits for them, and re-layouts: 29 us -> 16.5 us
where the time goes in v2:
time: 446 us
  Pallas kernels  428 us (96%)
  local copies, waits for them, and re-layouts  16.5 us (4%)
    pallas_call x2, Pallas kernels, backward(): pl.pallas_call(functools.partial(backward_body, tile, unroll, last), grid...  236 us
    pallas_call x1, Pallas kernels, update(): pl.pallas_call(functools.partial(update_body, count), in_specs=[ANY] * 12...  143 us
    pallas_call x1, Pallas kernels, forward(): pl.pallas_call(forward_body, grid=(tokens // tile,), in_specs=[rows, rows...  49.5 us
    unnamed x9, local copies, waits for them, and re-layouts  16.5 us

profile of v2, /device:TPU:112, one launch (start us, length us, event | category | flops | bytes accessed | tf_op | source)
XLA Modules:
  0.0 445.6 jit_solution(17198439574755510211)
XLA Ops:
  0.6 49.5 %forward.1 = (f32[7,4096,256]{2,1,0:T(8,128)}, f32[7,4096,256]{2,1,0:T(8,128)}, bf16[768,4096]{1,0:T(8,128)(2,1)}, bf16[4096,768]{1,0:T(8,128)(2,1)}, bf16[4096,...) custom-call(bf16[4096,768]{1,0:T(8,128)(2,1)} %bitcast.2, bf16[4096,768]{1,0:T(8,128)(2,1)} %bitcast.3, ...), custom_call_target="tpu_custom_call" | custom-call | flops 33822867456 | bytes 50331648 | tf_op jit(solution)/shard_map/forward/pallas_call | solution.py:119
  50.2 129.3 %backward_last.1 = (bf16[4096,768]{1,0:T(8,128)(2,1)}, bf16[768,4096]{1,0:T(8,128)(2,1)}, bf16[192,1792]{1,0:T(8,128)(2,1)}, bf16[192,1792]{1,0:T(8,128)(2,1)}, ...) custom-call(bf16[4096,768]{1,0:T(8,128)(2,1)} %get-tuple-element.29.refs_0_, ...), custom_call_target="tpu_custom_call" | custom-call | flops 90194313216 | bytes 50331648 | tf_op jit(solution)/shard_map/backward_last/pallas_call | solution.py:433
  179.5 106.3 %backward_first.1 = (bf16[2,192,1792]{2,1,0:T(8,128)(2,1)}, bf16[2,192,1792]{2,1,0:T(8,128)(2,1)}, bf16[2,448,768]{2,1,0:T(8,128)(2,1)}) custom-call(f32[7,4096,256]{2,1,0:T(8,128)} %get-tuple-element.26.refs_0_, f32[7,4096,256]{2,1,0:T(8,128)} %get-tuple-element.27.refs_1_, bf16[768,4096]{1,0:T(8,128)(2,1)} %get-tuple-element.28.refs_2_, ...), custom_call_target="tpu_custom_call" | custom-call | flops 45097156608 | bytes 50331648 | tf_op jit(solution)/shard_map/backward_first/pallas_call | solution.py:433
  285.8 143.2 %update.1 = (bf16[2,768,1792]{2,1,0:T(8,128)(2,1)S(1)}, bf16[2,768,1792]{2,1,0:T(8,128)(2,1)S(1)}, bf16[2,1792,768]{2,1,0:T(8,128)(2,1)S(1)}, f32[2,192,1792]{2,...) custom-call(bf16[2,192,1792]{2,1,0:T(8,128)(2,1)} %get-tuple-element, ...), custom_call_target="tpu_custom_call" | custom-call | tf_op jit(solution)/shard_map/update/pallas_call | solution.py:539
  429.0 2.4 copy.29
  431.5 1.5 copy.32
  433.0 1.5 copy.33
  434.6 1.5 copy.34
  436.1 1.5 copy.35
  437.6 1.5 copy.36
  439.2 1.5 copy.37
  440.7 2.4 copy.30
  443.1 2.4 copy.31

commit v3 on v2

v3 whole, which is shorter than its diff:
```python
import functools

import jax
import jax.numpy as jnp
from jax import lax
from jax.experimental import pallas as pl
from jax.experimental.pallas import tpu as pltpu
from jax.sharding import PartitionSpec as P

F32, BF16 = jnp.float32, jnp.bfloat16
VMEM_LIMIT = 66_000_000
CHUNK = 256
MESH = pl.DeviceIdType.MESH
ANY = pl.BlockSpec(memory_space=pl.ANY)


def dot(a, b):
    return jnp.dot(a, b, preferred_element_type=F32)


def dot_t(a, b):
    return lax.dot_general(a, b, (((1,), (1,)), ((), ())), preferred_element_type=F32)


def scale_of(wide):
    return lax.rsqrt(jnp.mean(wide * wide, -1, keepdims=True) + 1e-6)


def whole(shape, at=None):
    if at is None:
        return pl.BlockSpec(shape, lambda *_: (0,) * len(shape), pipeline_mode=pl.Buffered(1))
    return pl.BlockSpec((None, *shape), lambda *_: (at,) + (0,) * len(shape), pipeline_mode=pl.Buffered(1))


def ring():
    n = lax.axis_size("dp")
    me = lax.axis_index("dp")
    return me, (me + 1) % n, (me + n - 1) % n, (me + 2) % n


def meet(others):
    barrier = pltpu.get_barrier_semaphore()
    for other in others:
        pl.semaphore_signal(barrier, inc=1, device_id={"dp": other}, device_id_type=MESH)
    pl.semaphore_wait(barrier, len(others))


def remote(src, dst, send, recv, to):
    return pltpu.make_async_remote_copy(src_ref=src, dst_ref=dst, send_sem=send, recv_sem=recv, device_id={"dp": to}, device_id_type=MESH)


class Scatter:
    def __init__(self, piece, landed, final, send, recv):
        self.piece, self.landed, self.final = piece, landed, final
        self.me, right, left, far = ring()
        self.right, self.left = right, left
        self.routes = (
            lambda: (piece(far, 0), landed.at[0], right),
            lambda: (piece(far, 1), landed.at[1], left),
            lambda: (piece(right, 1), final.at[0, 1], right),
            lambda: (piece(left, 0), final.at[1, 0], left),
            lambda: (landed.at[0], final.at[0, 0], right),
            lambda: (landed.at[1], final.at[1, 1], left),
        )
        self.semaphores = send, recv

    def copy(self, k):
        src, dst, to = self.routes[k]()
        return remote(src, dst, self.semaphores[0].at[k], self.semaphores[1].at[k], to)

    def start(self):
        for k in range(4):
            self.copy(k).start()

    def middle(self):
        for k, own in enumerate((self.piece(self.right, 0), self.piece(self.left, 1))):
            self.copy(k).wait_recv()
            self.landed[k] = (self.landed[k].astype(F32) + own[...].astype(F32)).astype(BF16)
        for k in range(4, 6):
            self.copy(k).start()

    def finish(self, put):
        for k in range(2, 6):
            self.copy(k).wait_recv()
        for half in range(2):
            total = self.piece(self.me, half)[...].astype(F32) + self.final[0, half].astype(F32) + self.final[1, half].astype(F32)
            put(half, total.astype(BF16))
        for k in range(6):
            self.copy(k).wait_send()


def forward_body(x_ref, dy_ref, wg_ref, wu_ref, wd_ref, gate_ref, up_ref, hid_ref, at_ref, h_ref, a2_ref, a2t_ref, dyt_ref, hid):
    x = x_ref[...].astype(F32)
    a = (x * scale_of(x)).astype(BF16)
    for j in range(wg_ref.shape[1] // CHUNK):
        at = slice(j * CHUNK, (j + 1) * CHUNK)
        gate, up = dot(a, wg_ref[:, at]), dot(a, wu_ref[:, at])
        gate_ref[j], up_ref[j] = gate, up
        hid[:, at] = hid_ref[j] = (gate * jax.nn.sigmoid(gate) * up).astype(BF16)
    at_ref[...] = a.T
    dyt_ref[...] = dy_ref[...].T
    h = (x + dot(hid[...], wd_ref[...]).astype(BF16).astype(F32)).astype(BF16)
    h_ref[...] = h
    wide = h.astype(F32)
    a2 = (wide * scale_of(wide)).astype(BF16)
    a2_ref[...] = a2
    a2t_ref[...] = a2.T


def forward(x, dy, wg, wu, wd, layer, tile=512):
    tokens, d = x.shape
    ff = wg.shape[2]
    chunks = ff // CHUNK
    rows = pl.BlockSpec((tile, d), lambda i: (i, 0))
    columns = pl.BlockSpec((d, tile), lambda i: (0, i))
    kept = pl.BlockSpec((chunks, tile, CHUNK), lambda i: (0, i, 0))
    flat, turned = jax.ShapeDtypeStruct((tokens, d), BF16), jax.ShapeDtypeStruct((d, tokens), BF16)
    by_chunk = (chunks, tokens, CHUNK)
    return pl.pallas_call(
        forward_body,
        grid=(tokens // tile,),
        in_specs=[rows, rows, whole((d, ff), layer), whole((d, ff), layer), whole((ff, d), layer)],
        out_specs=[kept, kept, kept, columns, rows, rows, columns, columns],
        out_shape=[*(jax.ShapeDtypeStruct(by_chunk, t) for t in (F32, F32, BF16)), turned, flat, flat, turned, turned],
        scratch_shapes=[pltpu.VMEM((tile, ff), BF16)],
        compiler_params=pltpu.CompilerParams(vmem_limit_bytes=VMEM_LIMIT),
        cost_estimate=pl.CostEstimate(flops=6 * tokens * d * ff, bytes_accessed=16 * tokens * d, transcendentals=tokens * ff),
        name="forward",
    )(x, dy, wg, wu, wd)


def of(n):
    return lambda i: (2 * i) % n


def aligned(start, length, unit):
    return pl.ds(pl.multiple_of(start, unit), length)


def pair_job(ref, slot, landed, final, send, recv):
    part = landed.shape[-2]
    return Scatter(lambda owner, half: ref.at[:, aligned((2 * owner + half) * part, part, 32), :], landed.at[slot], final.at[slot], send.at[slot], recv.at[slot])


def put_pair(gg, gu, layer, chunk):
    def put(half, value):
        part = value.shape[1]
        at = (*layer, slice(half * part, (half + 1) * part), aligned(chunk * CHUNK, CHUNK, CHUNK))
        gg[at], gu[at] = value[0], value[1]

    return put


def down_job(ref, start, slot, landed, final, send, recv):
    part = landed.shape[-2]
    return Scatter(lambda owner, half: ref.at[aligned(start(owner) + half * part, part, 16), :], landed.at[slot], final.at[slot], send.at[slot], recv.at[slot])


def put_down(gd, layer, start):
    def put(half, value):
        part = value.shape[0]
        gd[(*layer, aligned(start + half * part, part, 16), slice(None))] = value

    return put


def left_over(owner, b, share):
    short = 2 * CHUNK - share
    return b * short + (1 - (owner - b + 3) // 4) * CHUNK


def gradients_of(gate, up, dhid):
    sig = jax.nn.sigmoid(gate)
    silu = gate * sig
    return (silu * up).astype(BF16), (dhid * up * (sig + silu * (1 - sig))).astype(BF16), (dhid * silu).astype(BF16)


def last_body(tile, unroll, *refs):
    a_in, at_in, dy_in, dyt_in, wg_ref, wu_ref, wd_ref, h_ref, dh_ref, dht_ref, gg, gu, gd, pair, down, a_ref, at_ref, dy_ref, dyt_ref, loads, gw, uw, dw, *rest = refs
    (*pairs, landed1, final1, send1, recv1, da, h, h_sem, out_sem) = rest
    tokens, d = dy_ref.shape
    share = gd.shape[0]
    i, chunks = pl.program_id(0), pl.num_programs(0)
    order = of(chunks)
    me, right, left, far = ring()
    n_tiles = tokens // tile
    wg, wu, wd = wg_ref[...], wu_ref[...], wd_ref[...]
    wgu = jnp.concatenate([wg, wu], 1)

    def own(number):
        return pair_job(pair, number, *pairs)

    def evens():
        return down_job(down, lambda owner: owner * 2 * CHUNK, 0, landed1, final1, send1, recv1)

    def rows_of(t):
        return aligned(t * tile, tile, tile)

    def load(t):
        by_rows, by_columns = (rows_of(t), slice(None)), (slice(None), rows_of(t))
        arrays = (dy_in, dy_ref, by_rows), (a_in, a_ref, by_rows), (at_in, at_ref, by_columns), (dyt_in, dyt_ref, by_columns)
        return [pltpu.make_async_copy(src.at[at], dst.at[at], loads.at[k, t]) for k, (src, dst, at) in enumerate(arrays)]

    def fetch(t, slot):
        return pltpu.make_async_copy(h_ref.at[rows_of(t), :], h.at[slot], h_sem.at[slot])

    def hand_on(t):
        by_rows, by_columns = (rows_of(t), slice(None)), (slice(None), rows_of(t))
        return [
            pltpu.make_async_copy(dy_ref.at[by_rows], dh_ref.at[by_rows], out_sem.at[0, t]),
            pltpu.make_async_copy(dyt_ref.at[by_columns], dht_ref.at[by_columns], out_sem.at[1, t]),
        ]

    def step(t, ends=False):
        rows = rows_of(t)
        a, dy = a_ref[rows, :], dy_ref[rows, :]
        hid, dgate, dup = gradients_of(dot(a, wg), dot(a, wu), dot_t(dy, wd).astype(BF16).astype(F32))
        at, dyt = at_ref[:, rows], dyt_ref[:, rows]
        dw[...] += dot(dyt, hid)
        uw[...] += dot(at, dup)
        gw[...] += dot(at, dgate)
        da_t = dot_t(jnp.concatenate([dgate, dup], 1), wgu)
        if not ends:
            da[rows, :] = jnp.where(i == 0, da_t, da[rows, :] + da_t)
        else:
            wide = h[t % 2].astype(F32)
            scale = scale_of(wide)
            back = (da[rows, :] + da_t).astype(BF16).astype(F32)
            coefficient = jnp.sum(back * wide, -1, keepdims=True) * (scale * scale * scale) * (1.0 / wide.shape[1])
            through = (back * scale - wide * coefficient).astype(BF16)
            dh = (dy.astype(F32) + through.astype(F32)).astype(BF16)
            dy_ref[rows, :] = dh
            dyt_ref[:, rows] = dh.T

    def steps(start, stop):
        def some(m, carry):
            @pl.when(i == 0)
            def _():
                for k in range(unroll):
                    for copy in load(m * unroll + k):
                        copy.wait()

            for k in range(unroll):
                step(m * unroll + k)
            return carry

        def some_last(t, carry):
            fetch(t, t % 2).wait()

            @pl.when(t + 1 < n_tiles)
            def _():
                fetch(t + 1, (t + 1) % 2).start()

            @pl.when(t > 0)
            def _():
                for copy in hand_on(t - 1):
                    copy.start()

            step(t, ends=True)
            return carry

        @pl.when(i < chunks - 1)
        def _():
            lax.fori_loop(start // unroll, stop // unroll, some, 0)

        @pl.when(i == chunks - 1)
        def _():
            if start == 0:
                fetch(0, 0).start()
            lax.fori_loop(start, stop, some_last, 0)

    for total in (gw, uw, dw):
        total[...] = jnp.zeros_like(total)

    @pl.when(i == 0)
    def _():
        for t in range(n_tiles):
            for copy in load(t):
                copy.start()
        meet((right, left))

    @pl.when(i > 0)
    def _():
        own(i - 1).start()

    steps(0, n_tiles // 2)

    @pl.when(i > 0)
    def _():
        own(i - 1).middle()

    @pl.when(i == 4)
    def _():
        evens().start()

    @pl.when(i == 5)
    def _():
        evens().middle()

    @pl.when(i == 6)
    def _():
        evens().finish(put_down(gd, (), me * (2 * CHUNK - share)))

    steps(n_tiles // 2, n_tiles)

    @pl.when(i > 0)
    def _():
        own(i - 1).finish(put_pair(gg, gu, (), order(i - 1)))

    pair[0] = gw[...].astype(BF16)
    pair[1] = uw[...].astype(BF16)
    down[aligned(order(i) * CHUNK, CHUNK, CHUNK), :] = dw[...].astype(BF16).T

    @pl.when(i == chunks - 1)
    def _():
        for copy in hand_on(n_tiles - 1):
            copy.start()
        for t in range(n_tiles):
            for copy in hand_on(t):
                copy.wait()


def first_body(tile, unroll, *refs):
    gate_in, up_in, hid_ref, at_in, dy_in, dyt_in, wd_ref, gg_in, gu_in, gd_in, pair_in, down_hbm, gg, gu, gd, pair, down, down_in, kept, kept_sem, g_sem, at_ref, dy_ref, dyt_ref, loads, gw, uw, by, *rest = refs
    pairs, downs, leftovers = rest[:4], rest[4:8], rest[8:]
    tokens, d = dy_ref.shape
    share = gd.shape[-2]
    i, chunks = pl.program_id(0), down.shape[0] // CHUNK
    n = i - chunks
    me, right, left, far = ring()
    n_tiles = tokens // tile
    runs = downs[0].shape[0]
    run = share // runs

    def held(row):
        return row // (2 * CHUNK) * CHUNK + row % CHUNK

    def odd_chunks():
        return [
            pltpu.make_async_copy(down_hbm.at[(2 * b + 1) * CHUNK : (2 * b + 2) * CHUNK, :], down_in.at[b * CHUNK : (b + 1) * CHUNK, :], g_sem.at[3 + b])
            for b in range(chunks // 2)
        ]

    def before():
        jobs = [(pair_job(pair_in, chunks, *pairs), put_pair(gg, gu, (1,), of(chunks)(chunks - 1)))]
        for b in range(3):
            start = functools.partial(left_over, b=b, share=share)
            jobs.append((down_job(down_in, lambda owner, start=start: held(owner * share + start(owner)), b, *leftovers), put_down(gd, (1,), start(me))))
        return jobs

    def own(number):
        return pair_job(pair.at[number % 3], number, *pairs), put_pair(gg, gu, (0,), number)

    def rows_job(number):
        return down_job(down, lambda owner: owner * share + number * run, number, *downs), put_down(gd, (0,), number * run)

    def rows_of(t):
        return aligned(t * tile, tile, tile)

    def load(k, t):
        by_rows, by_columns = (rows_of(t), slice(None)), (slice(None), rows_of(t))
        src, dst, at = ((dyt_in, dyt_ref, by_columns), (dy_in, dy_ref, by_rows), (at_in, at_ref, by_columns))[k]
        return pltpu.make_async_copy(src.at[at], dst.at[at], loads.at[k, t])

    def keep(number):
        return [pltpu.make_async_copy(src.at[number], kept.at[number % 2, k], kept_sem.at[number % 2, k]) for k, src in enumerate((gate_in, up_in))]

    def g_before():
        return [pltpu.make_async_copy(src, dst.at[1], g_sem.at[k]) for k, (src, dst) in enumerate(((gg_in, gg), (gu_in, gu), (gd_in, gd)))]

    @pl.when(i == 0)
    def _():
        for copy in odd_chunks() + [load(0, t) for t in range(n_tiles)] + g_before() + [load(k, t) for t in range(n_tiles) for k in (1, 2)] + keep(0):
            copy.start()
        meet((right, left))
        for copy in odd_chunks():
            copy.wait()
        for job, _ in before():
            job.start()

    @pl.when(i == 4)
    def _():
        before()[0][0].middle()

    @pl.when(i == 6)
    def _():
        for copy in g_before():
            copy.wait()
        jobs = before()
        for job, _ in jobs[1:]:
            job.middle()
        jobs[0][0].finish(jobs[0][1])

    @pl.when(i == chunks + 1)
    def _():
        for job, put in before()[1:]:
            job.finish(put)

    @pl.when(n < 0)
    def _():
        gw[...] = jnp.zeros_like(gw)

        def some(t, carry):
            @pl.when(i == 0)
            def _():
                for k in range(unroll):
                    load(0, t * unroll + k).wait()

            rows = pl.ds(pl.multiple_of(t * tile * unroll, tile * unroll), tile * unroll)
            gw[...] += dot(dyt_ref[:, rows], hid_ref[rows, :])
            return carry

        lax.fori_loop(0, n_tiles // unroll, some, 0)
        down[aligned(i * CHUNK, CHUNK, CHUNK), :] = gw[...].astype(BF16).T

    @pl.when(n >= 1)
    def _():
        own(n - 1)[0].start()

    for b in range(2):

        @pl.when(n == b)
        def _():
            rows_job(b)[0].start()

    @pl.when(n >= 2)
    def _():
        own(n - 2)[0].middle()

    for b in range(2):

        @pl.when(n == b + 2)
        def _():
            rows_job(b)[0].middle()

    @pl.when(n >= 3)
    def _():
        job, put = own(n - 3)
        job.finish(put)

    for b in range(2):

        @pl.when(n == b + 4)
        def _():
            job, put = rows_job(b)
            job.finish(put)

    @pl.when(n >= 0)
    def _():
        @pl.when(n + 1 < chunks)
        def _():
            for copy in keep(n + 1):
                copy.start()

        gw[...] = jnp.zeros_like(gw)
        uw[...] = jnp.zeros_like(uw)
        wd = wd_ref[...]
        for copy in keep(n):
            copy.wait()
        slot = n % 2

        def some(m, carry):
            @pl.when(n == 0)
            def _():
                for k in range(unroll):
                    for which in (1, 2):
                        load(which, m * unroll + k).wait()

            for k in range(unroll):
                rows = rows_of(m * unroll + k)
                dhid = dot_t(dy_ref[rows, :], wd).astype(BF16).astype(F32)
                _, dgate, dup = gradients_of(kept[slot, 0, rows, :], kept[slot, 1, rows, :], dhid)
                by[0, k * tile : (k + 1) * tile, :] = dgate
                by[1, k * tile : (k + 1) * tile, :] = dup
            at = at_ref[:, aligned(m * unroll * tile, unroll * tile, unroll * tile)]
            gw[...] += dot(at, by[0])
            uw[...] += dot(at, by[1])
            return carry

        lax.fori_loop(0, n_tiles // unroll, some, 0)
        pair[n % 3, 0] = gw[...].astype(BF16)
        pair[n % 3, 1] = uw[...].astype(BF16)

    @pl.when(n == chunks - 1)
    def _():
        ends = [own(chunks - 3 + k) for k in range(3)]
        ends[2][0].start()
        ends[1][0].middle()
        ends[0][0].finish(ends[0][1])
        ends[2][0].middle()
        for job, put in ends[1:]:
            job.finish(put)


def scatter_scratch(jobs, *half):
    dma = pltpu.SemaphoreType.DMA
    return [pltpu.VMEM((jobs, 2, *half), BF16), pltpu.VMEM((jobs, 2, 2, *half), BF16), dma((jobs, 6)), dma((jobs, 6))]


def shares(w, group):
    _, d, ff = w[0].shape
    return [(d // group, ff), (d // group, ff), (ff // group, d)]


def backward_last(a, at, dy, dyt, w, layer, h, group, tile=512, unroll=1):
    tokens, d = dy.shape
    _, _, ff = w[0].shape
    chunks = ff // CHUNK
    by_columns = pl.BlockSpec((None, d, CHUNK), lambda i: (layer, 0, of(chunks)(i)))
    by_rows = pl.BlockSpec((None, CHUNK, d), lambda i: (layer, of(chunks)(i), 0))
    shapes = shares(w, group) + [(2, d, CHUNK), (ff, d)]
    dma = pltpu.SemaphoreType.DMA
    scratch = [pltpu.VMEM((tokens, d), BF16), pltpu.VMEM((d, tokens), BF16)] * 2 + [dma((4, tokens // tile))]
    scratch += [pltpu.VMEM((d, CHUNK), F32)] * 3
    scratch += scatter_scratch(chunks - 1, 2, d // group // 2, CHUNK) + scatter_scratch(1, CHUNK // 2, d)
    scratch += [pltpu.VMEM((tokens, d), F32), pltpu.VMEM((2, tile, d), BF16), dma((2,)), dma((2, tokens // tile))]
    return pl.pallas_call(
        functools.partial(last_body, tile, unroll),
        grid=(chunks,),
        in_specs=[ANY] * 4 + [by_columns, by_columns, by_rows, ANY],
        out_specs=[ANY, ANY] + [whole(s) for s in shapes],
        out_shape=[jax.ShapeDtypeStruct(s, BF16) for s in ((tokens, d), (d, tokens), *shapes)],
        scratch_shapes=scratch,
        compiler_params=pltpu.CompilerParams(vmem_limit_bytes=VMEM_LIMIT, collective_id=1, has_side_effects=True),
        cost_estimate=pl.CostEstimate(flops=16 * tokens * d * ff, bytes_accessed=16 * tokens * d, transcendentals=tokens * ff),
        name="backward_last",
    )(a, at, dy, dyt, *w, h)


def backward_first(gate, up, hid, at, dy, dyt, w, layer, before, group, tile=512, unroll=4):
    tokens, d = dy.shape
    layers, _, ff = w[0].shape
    chunks = ff // CHUNK
    by_chunk = pl.BlockSpec((None, tokens, CHUNK), lambda i: (jnp.minimum(i, chunks - 1), 0, 0))
    by_rows = pl.BlockSpec((None, CHUNK, d), lambda i: (layer, jnp.maximum(i - chunks, 0), 0))
    shapes = [(layers, *s) for s in shares(w, group)]
    dma = pltpu.SemaphoreType.DMA
    short = 2 * CHUNK - ff // group
    scratch = [pltpu.VMEM((3, 2, d, CHUNK), BF16), pltpu.VMEM((ff, d), BF16), pltpu.VMEM((chunks // 2 * CHUNK, d), BF16)]
    scratch += [pltpu.VMEM((2, 2, tokens, CHUNK), F32), dma((2, 2)), dma((3 + chunks // 2,))]
    scratch += [pltpu.VMEM((d, tokens), BF16), pltpu.VMEM((tokens, d), BF16), pltpu.VMEM((d, tokens), BF16), dma((3, tokens // tile))]
    scratch += [pltpu.VMEM((d, CHUNK), F32)] * 2 + [pltpu.VMEM((2, unroll * tile, CHUNK), BF16)]
    scratch += scatter_scratch(chunks + 1, 2, d // group // 2, CHUNK) + scatter_scratch(2, ff // group // 4, d) + scatter_scratch(3, short // 2, d)
    return pl.pallas_call(
        functools.partial(first_body, tile, unroll),
        grid=(2 * chunks,),
        in_specs=[ANY, ANY, by_chunk] + [ANY] * 3 + [by_rows] + [ANY] * 3 + [whole((2, d, CHUNK)), ANY],
        out_specs=[whole(s) for s in shapes],
        out_shape=[jax.ShapeDtypeStruct(s, BF16) for s in shapes],
        scratch_shapes=scratch,
        compiler_params=pltpu.CompilerParams(vmem_limit_bytes=VMEM_LIMIT, collective_id=2, has_side_effects=True),
        cost_estimate=pl.CostEstimate(flops=8 * tokens * d * ff, bytes_accessed=16 * tokens * d, transcendentals=tokens * ff),
        name="backward_first",
    )(gate, up, hid, at, dy, dyt, w[2], *before)


def adamw(w, m, v, g):
    m = 0.9 * m + 0.1 * g
    v = 0.95 * v + 0.05 * g * g
    step = m * lax.rsqrt(v + 1e-8) + 0.1 * w
    return (w - 0.02 * step).astype(BF16), m, v


def update_body(count, *refs):
    g_in, w, m, v, new_w, new_m, new_v, g = (refs[k : k + 3] for k in range(0, 24, 3))
    mine, sums, norm_send, norm_recv, load, send, recv = refs[24:]
    me, right, left, far = ring()
    layers = g[0].shape[0]
    loads = {}

    def fetch(which, k, layer, src, dst, at):
        loads[k, layer, which] = pltpu.make_async_copy(src[k].at[at], dst[k].at[at], load.at[k, layer, which])
        loads[k, layer, which].start()

    parts = [(k, layer) for k in range(3) for layer in range(layers)]
    for k, layer in parts:
        fetch(3, k, layer, g_in, g, layer)
    for k, layer in parts:
        fetch(0, k, layer, w, new_w, (layer, pl.ds(pl.multiple_of(me * g[k].shape[1], 32), g[k].shape[1])))
        fetch(1, k, layer, m, new_m, layer)
        fetch(2, k, layer, v, new_v, layer)
    meet((right, left, far))
    total = jnp.float32(0)
    for k in range(3):
        for layer in range(layers):
            loads[k, layer, 3].wait()

            def add(r, squares):
                part = g[k][layer, pl.ds(pl.multiple_of(r * 16, 16), 16), :].astype(F32)
                return squares + part * part

            total += jnp.sum(lax.fori_loop(0, g[k].shape[1] // 16, add, jnp.zeros((16, g[k].shape[2]), F32)))
    mine[...] = jnp.full(mine.shape, total, F32)
    sums[me] = mine[...]
    tells = [remote(mine, sums.at[me], norm_send.at[n], norm_recv.at[n], to) for n, to in enumerate((right, left, far))]
    for tell in tells:
        tell.start()
    for tell in tells:
        tell.wait()
    squares = sum(sums[n] for n in range(sums.shape[0]))
    factor = jnp.minimum(1.0, 0.5 * lax.rsqrt(squares / count + 1e-30))[0:1, 0:1]

    copies = []
    for k in range(3):
        size, rows = g[k].shape[1], 32
        half = size // 2
        for layer in range(layers):
            for which in range(3):
                loads[k, layer, which].wait()

            def change(r, carry):
                at = (layer, pl.ds(pl.multiple_of(r * rows, rows), rows), slice(None))
                own = (layer, pl.ds(pl.multiple_of(me * size + r * rows, rows), rows), slice(None))
                new = adamw(new_w[k][own].astype(F32), new_m[k][at], new_v[k][at], g[k][at].astype(F32) * factor)
                new_w[k][own], new_m[k][at], new_v[k][at] = new
                return carry

            lax.fori_loop(0, size // rows, change, 0)

            def block(owner, start, length):
                return new_w[k].at[layer, pl.ds(pl.multiple_of(owner * size + start, 32), length), :]

            s, r = send.at[k, layer], recv.at[k, layer]
            direct = [remote(block(me, 0, size), block(me, 0, size), s.at[n], r.at[n], to) for n, to in enumerate((right, left))]
            on = [
                remote(block(left, 0, half), block(left, 0, half), s.at[2], r.at[2], right),
                remote(block(right, half, half), block(right, half, half), s.at[3], r.at[3], left),
            ]
            for copy in direct:
                copy.start()
            copies.append((direct, on))
    for direct, on in copies:
        for first, second in zip(direct, on, strict=True):
            first.wait_recv()
            second.start()
    for direct, on in copies:
        for copy in on:
            copy.wait()
        for copy in direct:
            copy.wait_send()


def update(g, w, m, v):
    count = sum(t.size for t in w)
    layers = w[0].shape[0]
    shapes = [pltpu.VMEM(t.shape, t.dtype) for t in (*w, *m, *v)]
    dma = pltpu.SemaphoreType.DMA
    group = w[0].shape[1] // m[0].shape[1]
    vmem = pl.BlockSpec(memory_space=pltpu.VMEM)
    return pl.pallas_call(
        functools.partial(update_body, count),
        in_specs=[ANY] * 12,
        out_specs=[vmem] * 9,
        out_shape=shapes,
        scratch_shapes=[pltpu.VMEM(t.shape, BF16) for t in m]
        + [pltpu.VMEM((8, 128), F32), pltpu.VMEM((group, 8, 128), F32), dma((3,)), dma((3,))]
        + [dma((3, layers, 4)), dma((3, layers, 4)), dma((3, layers, 4))],
        compiler_params=pltpu.CompilerParams(vmem_limit_bytes=28_000_000, collective_id=3, has_side_effects=True),
        name="update",
    )(*g, *w, *m, *v)


def deliver_body(*refs):
    copies = [pltpu.make_async_copy(refs[k], refs[9 + k], refs[18].at[k]) for k in range(9)]
    for copy in copies:
        copy.start()
    for copy in copies:
        copy.wait()


def deliver(arrays):
    arrays = [pltpu.with_memory_space_constraint(t, pltpu.VMEM) for t in arrays]
    return pl.pallas_call(
        deliver_body,
        in_specs=[pl.BlockSpec(memory_space=pltpu.VMEM)] * 9,
        out_specs=[ANY] * 9,
        out_shape=[jax.ShapeDtypeStruct(t.shape, t.dtype) for t in arrays],
        scratch_shapes=[pltpu.SemaphoreType.DMA((9,))],
        compiler_params=pltpu.CompilerParams(vmem_limit_bytes=28_000_000),
        name="deliver",
    )(*arrays)


def solution(mesh):
    group = mesh.shape["dp"]

    def step(x, dy, *arrays):
        w, m, v = (arrays[i : i + 3] for i in (0, 3, 6))
        x, dy = x[0], dy[0]
        gate, up, hid, a1t, h1, a2, a2t, dyt = forward(x, dy, *w, 0)
        dh, dht, *before = backward_last(a2, a2t, dy, dyt, w, 1, h1, group)
        g = backward_first(gate, up, hid, a1t, dh, dht, w, 0, before, group)
        return tuple(deliver(update(g, w, m, v)))

    sequence, rows = P(("rep", "dp"), None, None), P(None, "dp", None)
    return jax.shard_map(
        step,
        mesh=mesh,
        in_specs=(sequence,) * 2 + (P(),) * 3 + (rows,) * 6,
        out_specs=(P("rep", None, None),) * 3 + (P("rep", "dp", None),) * 6,
        check_vma=False,
    )
```

time: 446 us -> 433 us (0.971)
  local copies, waits for them, and re-layouts: 16.5 us -> 0 us
    unnamed x9 -> x0, local copies, waits for them, and re-layouts: 16.5 us -> none
    pallas_call x2 -> x3, Pallas kernels: 236 us -> 239 us  [the longest x1 129 us: backward_last(): pl.pallas_call(functools.partial(last_body, tile, unroll), grid=(chunks,)...]
where the time goes in v3:
time: 433 us
  Pallas kernels  432 us (100%)
    pallas_call x1, Pallas kernels, update(): pl.pallas_call(functools.partial(update_body, count), in_specs=[ANY] * 12...  143 us
    pallas_call x1, Pallas kernels, backward_last(): pl.pallas_call(functools.partial(last_body, tile, unroll), grid=(chunks,)...  129 us
    pallas_call x1, Pallas kernels, backward_first(): pl.pallas_call(functools.partial(first_body, tile, unroll), grid=(2 * chu...  99.4 us
    pallas_call x1, Pallas kernels, forward(): pl.pallas_call(forward_body, grid=(tokens // tile,), in_specs=[rows, rows...  50.1 us
    pallas_call x1, Pallas kernels, deliver(): pl.pallas_call(deliver_body, in_specs=[pl.BlockSpec(memory_space=pltpu.VM...  10.9 us

profile of v3, /device:TPU:112, one launch (start us, length us, event | category | flops | bytes accessed | tf_op | source)
XLA Modules:
  0.0 433.0 jit_solution(18394147870518617180)
XLA Ops:
  0.6 50.1 %forward.1 = (f32[7,4096,256]{2,1,0:T(8,128)}, f32[7,4096,256]{2,1,0:T(8,128)}, bf16[7,4096,256]{2,1,0:T(8,128)(2,1)}, bf16[768,4096]{1,0:T(8,128)(2,1)}, bf16[4...) custom-call(bf16[4096,768]{1,0:T(8,128)(2,1)} %bitcast.2, ...), custom_call_target="tpu_custom_call" | custom-call | flops 33822867456 | bytes 50331648 | tf_op jit(solution)/shard_map/forward/pallas_call | solution.py:119
  50.7 128.5 %backward_last.1 = (bf16[4096,768]{1,0:T(8,128)(2,1)}, bf16[768,4096]{1,0:T(8,128)(2,1)}, bf16[192,1792]{1,0:T(8,128)(2,1)}, bf16[192,1792]{1,0:T(8,128)(2,1)}, ...) custom-call(bf16[4096,768]{1,0:T(8,128)(2,1)} %get-tuple-element.40.refs_0_, ...), custom_call_target="tpu_custom_call" | custom-call | flops 90194313216 | bytes 50331648 | tf_op jit(solution)/shard_map/backward_last/pallas_call | solution.py:517
  179.3 99.4 %backward_first.1 = (bf16[2,192,1792]{2,1,0:T(8,128)(2,1)}, bf16[2,192,1792]{2,1,0:T(8,128)(2,1)}, bf16[2,448,768]{2,1,0:T(8,128)(2,1)}) custom-call(f32[7,4096,256]{2,1,0:T(8,128)} %get-tuple-element.36.refs_0_, f32[7,4096,256]{2,1,0:T(8,128)} %get-tuple-element.37.refs_1_, bf16[7,4096,256]{2,1,0:T(8,128)(2,1)} %get-tuple-element.38.refs_2_, ...), custom_call_target="tpu_custom_call" | custom-call | flops 45097156608 | bytes 50331648 | tf_op jit(solution)/shard_map/backward_first/pallas_call | solution.py:544
  278.7 143.2 %update.1 = (bf16[2,768,1792]{2,1,0:T(8,128)(2,1)S(1)}, bf16[2,768,1792]{2,1,0:T(8,128)(2,1)S(1)}, bf16[2,1792,768]{2,1,0:T(8,128)(2,1)S(1)}, f32[2,192,1792]{2,...) custom-call(bf16[2,192,1792]{2,1,0:T(8,128)(2,1)} %get-tuple-element, ...), custom_call_target="tpu_custom_call" | custom-call | tf_op jit(solution)/shard_map/update/pallas_call | solution.py:650
  422.0 10.9 %deliver.1 = (bf16[2,768,1792]{2,1,0:T(8,128)(2,1)}, bf16[2,768,1792]{2,1,0:T(8,128)(2,1)}, bf16[2,1792,768]{2,1,0:T(8,128)(2,1)}, f32[2,192,1792]{2,1,0:T(8,128...) custom-call(bf16[2,768,1792]{2,1,0:T(8,128)(2,1)S(1)} %get-tuple-ele, ...), custom_call_target="tpu_custom_call" | custom-call | tf_op jit(solution)/shard_map/deliver/pallas_call | solution.py:673

commit v4 on v3

--- a/solution.py
+++ b/solution.py
@@ -97,14 +97,14 @@
         gate, up = dot(a, wg_ref[:, at]), dot(a, wu_ref[:, at])
         gate_ref[j], up_ref[j] = gate, up
         hid[:, at] = hid_ref[j] = (gate * jax.nn.sigmoid(gate) * up).astype(BF16)
-    at_ref[...] = a.T
-    dyt_ref[...] = dy_ref[...].T
     h = (x + dot(hid[...], wd_ref[...]).astype(BF16).astype(F32)).astype(BF16)
     h_ref[...] = h
     wide = h.astype(F32)
     a2 = (wide * scale_of(wide)).astype(BF16)
     a2_ref[...] = a2
     a2t_ref[...] = a2.T
+    at_ref[...] = a.T
+    dyt_ref[...] = dy_ref[...].T
 
 
 def forward(x, dy, wg, wu, wd, layer, tile=512):
@@ -175,6 +175,14 @@
     return (silu * up).astype(BF16), (dhid * up * (sig + silu * (1 - sig))).astype(BF16), (dhid * silu).astype(BF16)
 
 
+def squares_of(ref, layer):
+    def add(r, squares):
+        part = ref[layer, pl.ds(pl.multiple_of(r * 16, 16), 16), :].astype(F32)
+        return squares + part * part
+
+    return jnp.sum(lax.fori_loop(0, ref.shape[1] // 16, add, jnp.zeros((16, ref.shape[2]), F32)))
+
+
 def last_body(tile, unroll, *refs):
     a_in, at_in, dy_in, dyt_in, wg_ref, wu_ref, wd_ref, h_ref, dh_ref, dht_ref, gg, gu, gd, pair, down, a_ref, at_ref, dy_ref, dyt_ref, loads, gw, uw, dw, *rest = refs
     (*pairs, landed1, final1, send1, recv1, da, h, h_sem, out_sem) = rest
@@ -217,11 +225,11 @@
         hid, dgate, dup = gradients_of(dot(a, wg), dot(a, wu), dot_t(dy, wd).astype(BF16).astype(F32))
         at, dyt = at_ref[:, rows], dyt_ref[:, rows]
         dw[...] += dot(dyt, hid)
+        da_t = dot_t(jnp.concatenate([dgate, dup], 1), wgu)
         uw[...] += dot(at, dup)
         gw[...] += dot(at, dgate)
-        da_t = dot_t(jnp.concatenate([dgate, dup], 1), wgu)
         if not ends:
-            da[rows, :] = jnp.where(i == 0, da_t, da[rows, :] + da_t)
+            da[rows, :] += da_t
         else:
             wide = h[t % 2].astype(F32)
             scale = scale_of(wide)
@@ -272,11 +280,16 @@
     for total in (gw, uw, dw):
         total[...] = jnp.zeros_like(total)
 
+    def clear(t, carry):
+        da[rows_of(t), :] = jnp.zeros((tile, d), F32)
+        return carry
+
     @pl.when(i == 0)
     def _():
         for t in range(n_tiles):
             for copy in load(t):
                 copy.start()
+        lax.fori_loop(0, n_tiles, clear, 0)
         meet((right, left))
 
     @pl.when(i > 0)
@@ -321,7 +334,7 @@
 
 
 def first_body(tile, unroll, *refs):
-    gate_in, up_in, hid_ref, at_in, dy_in, dyt_in, wd_ref, gg_in, gu_in, gd_in, pair_in, down_hbm, gg, gu, gd, pair, down, down_in, kept, kept_sem, g_sem, at_ref, dy_ref, dyt_ref, loads, gw, uw, by, *rest = refs
+    gate_in, up_in, hid_ref, at_in, dy_in, dyt_in, wd_ref, gg_in, gu_in, gd_in, pair_in, down_hbm, gg, gu, gd, squares, pair, down, down_in, kept, kept_sem, g_sem, at_ref, dy_ref, dyt_ref, loads, gw, uw, by, *rest = refs
     pairs, downs, leftovers = rest[:4], rest[4:8], rest[8:]
     tokens, d = dy_ref.shape
     share = gd.shape[-2]
@@ -444,6 +457,10 @@
         def _():
             job, put = rows_job(b)
             job.finish(put)
+
+    @pl.when(n == 4)
+    def _():
+        squares[...] = jnp.full(squares.shape, sum(squares_of(ref, 1) for ref in (gg, gu, gd)), F32)
 
     @pl.when(n >= 0)
     def _():
@@ -490,6 +507,7 @@
         ends[2][0].middle()
         for job, put in ends[1:]:
             job.finish(put)
+        squares[...] += sum(squares_of(ref, 0) for ref in (gg, gu, gd))
 
 
 def scatter_scratch(jobs, *half):
@@ -545,8 +563,8 @@
         functools.partial(first_body, tile, unroll),
         grid=(2 * chunks,),
         in_specs=[ANY, ANY, by_chunk] + [ANY] * 3 + [by_rows] + [ANY] * 3 + [whole((2, d, CHUNK)), ANY],
-        out_specs=[whole(s) for s in shapes],
-        out_shape=[jax.ShapeDtypeStruct(s, BF16) for s in shapes],
+        out_specs=[whole(s) for s in (*shapes, (8, 128))],
+        out_shape=[jax.ShapeDtypeStruct(s, BF16) for s in shapes] + [jax.ShapeDtypeStruct((8, 128), F32)],
         scratch_shapes=scratch,
         compiler_params=pltpu.CompilerParams(vmem_limit_bytes=VMEM_LIMIT, collective_id=2, has_side_effects=True),
         cost_estimate=pl.CostEstimate(flops=8 * tokens * d * ff, bytes_accessed=16 * tokens * d, transcendentals=tokens * ff),
@@ -562,8 +580,9 @@
 
 
 def update_body(count, *refs):
+    mine, *refs = refs
     g_in, w, m, v, new_w, new_m, new_v, g = (refs[k : k + 3] for k in range(0, 24, 3))
-    mine, sums, norm_send, norm_recv, load, send, recv = refs[24:]
+    sums, norm_send, norm_recv, load, send, recv = refs[24:]
     me, right, left, far = ring()
     layers = g[0].shape[0]
     loads = {}
@@ -575,22 +594,10 @@
     parts = [(k, layer) for k in range(3) for layer in range(layers)]
     for k, layer in parts:
         fetch(3, k, layer, g_in, g, layer)
-    for k, layer in parts:
         fetch(0, k, layer, w, new_w, (layer, pl.ds(pl.multiple_of(me * g[k].shape[1], 32), g[k].shape[1])))
         fetch(1, k, layer, m, new_m, layer)
         fetch(2, k, layer, v, new_v, layer)
     meet((right, left, far))
-    total = jnp.float32(0)
-    for k in range(3):
-        for layer in range(layers):
-            loads[k, layer, 3].wait()
-
-            def add(r, squares):
-                part = g[k][layer, pl.ds(pl.multiple_of(r * 16, 16), 16), :].astype(F32)
-                return squares + part * part
-
-            total += jnp.sum(lax.fori_loop(0, g[k].shape[1] // 16, add, jnp.zeros((16, g[k].shape[2]), F32)))
-    mine[...] = jnp.full(mine.shape, total, F32)
     sums[me] = mine[...]
     tells = [remote(mine, sums.at[me], norm_send.at[n], norm_recv.at[n], to) for n, to in enumerate((right, left, far))]
     for tell in tells:
@@ -605,7 +612,7 @@
         size, rows = g[k].shape[1], 32
         half = size // 2
         for layer in range(layers):
-            for which in range(3):
+            for which in range(4):
                 loads[k, layer, which].wait()
 
             def change(r, carry):
@@ -640,7 +647,7 @@
             copy.wait_send()
 
 
-def update(g, w, m, v):
+def update(squares, g, w, m, v):
     count = sum(t.size for t in w)
     layers = w[0].shape[0]
     shapes = [pltpu.VMEM(t.shape, t.dtype) for t in (*w, *m, *v)]
@@ -649,15 +656,15 @@
     vmem = pl.BlockSpec(memory_space=pltpu.VMEM)
     return pl.pallas_call(
         functools.partial(update_body, count),
-        in_specs=[ANY] * 12,
+        in_specs=[vmem] + [ANY] * 12,
         out_specs=[vmem] * 9,
         out_shape=shapes,
         scratch_shapes=[pltpu.VMEM(t.shape, BF16) for t in m]
-        + [pltpu.VMEM((8, 128), F32), pltpu.VMEM((group, 8, 128), F32), dma((3,)), dma((3,))]
+        + [pltpu.VMEM((group, 8, 128), F32), dma((3,)), dma((3,))]
         + [dma((3, layers, 4)), dma((3, layers, 4)), dma((3, layers, 4))],
         compiler_params=pltpu.CompilerParams(vmem_limit_bytes=28_000_000, collective_id=3, has_side_effects=True),
         name="update",
-    )(*g, *w, *m, *v)
+    )(squares, *g, *w, *m, *v)
 
 
 def deliver_body(*refs):
@@ -689,8 +696,8 @@
         x, dy = x[0], dy[0]
         gate, up, hid, a1t, h1, a2, a2t, dyt = forward(x, dy, *w, 0)
         dh, dht, *before = backward_last(a2, a2t, dy, dyt, w, 1, h1, group)
-        g = backward_first(gate, up, hid, a1t, dh, dht, w, 0, before, group)
-        return tuple(deliver(update(g, w, m, v)))
+        *g, squares = backward_first(gate, up, hid, a1t, dh, dht, w, 0, before, group)
+        return tuple(deliver(update(squares, g, w, m, v)))
 
     sequence, rows = P(("rep", "dp"), None, None), P(None, "dp", None)
     return jax.shard_map(

time: 433 us -> 430 us (level)
  no operation moved by 1% of the time
where the time goes in v4:
time: 430 us
  Pallas kernels  429 us (100%)
    pallas_call x1, Pallas kernels, update(): pl.pallas_call(functools.partial(update_body, count), in_specs=[vmem] + [...  140 us
    pallas_call x1, Pallas kernels, backward_last(): pl.pallas_call(functools.partial(last_body, tile, unroll), grid=(chunks,)...  127 us
    pallas_call x1, Pallas kernels, backward_first(): pl.pallas_call(functools.partial(first_body, tile, unroll), grid=(2 * chu...  101 us
    pallas_call x1, Pallas kernels, forward(): pl.pallas_call(forward_body, grid=(tokens // tile,), in_specs=[rows, rows...  50.2 us
    pallas_call x1, Pallas kernels, deliver(): pl.pallas_call(deliver_body, in_specs=[pl.BlockSpec(memory_space=pltpu.VM...  10.9 us

profile of v4, /device:TPU:112, one launch (start us, length us, event | category | flops | bytes accessed | tf_op | source)
XLA Modules:
  0.0 430.1 jit_solution(5580928511781224890)
XLA Ops:
  0.6 50.2 %forward.1 = (f32[7,4096,256]{2,1,0:T(8,128)}, f32[7,4096,256]{2,1,0:T(8,128)}, bf16[7,4096,256]{2,1,0:T(8,128)(2,1)}, bf16[768,4096]{1,0:T(8,128)(2,1)}, bf16[4...) custom-call(bf16[4096,768]{1,0:T(8,128)(2,1)} %bitcast.2, ...), custom_call_target="tpu_custom_call" | custom-call | flops 33822867456 | bytes 50331648 | tf_op jit(solution)/shard_map/forward/pallas_call | solution.py:119
  50.9 127.3 %backward_last.1 = (bf16[4096,768]{1,0:T(8,128)(2,1)}, bf16[768,4096]{1,0:T(8,128)(2,1)}, bf16[192,1792]{1,0:T(8,128)(2,1)}, bf16[192,1792]{1,0:T(8,128)(2,1)}, ...) custom-call(bf16[4096,768]{1,0:T(8,128)(2,1)} %get-tuple-element.41.refs_0_, ...), custom_call_target="tpu_custom_call" | custom-call | flops 90194313216 | bytes 50331648 | tf_op jit(solution)/shard_map/backward_last/pallas_call | solution.py:535
  178.2 100.8 %backward_first.1 = (bf16[2,192,1792]{2,1,0:T(8,128)(2,1)}, bf16[2,192,1792]{2,1,0:T(8,128)(2,1)}, bf16[2,448,768]{2,1,0:T(8,128)(2,1)}, f32[8,128]{1,0:T(8,128)}) custom-call(f32[7,4096,256]{2,1,0:T(8,128)} %get-tuple-element.37.refs_0_, f32[7,4096,256]{2,1,0:T(8,128)} %get-tuple-element.38.refs_1_, bf16[7,4096,256]{2,1,0:T(8,128)(2,1)} %get-tuple-element.39.refs_2_, ...), custom_call_target="tpu_custom_call" | custom-call | flops 45097156608 | bytes 50331648 | tf_op jit(solution)/shard_map/backward_first/pallas_call | solution.py:562
  278.9 140.1 %update.1 = (bf16[2,768,1792]{2,1,0:T(8,128)(2,1)S(1)}, bf16[2,768,1792]{2,1,0:T(8,128)(2,1)S(1)}, bf16[2,1792,768]{2,1,0:T(8,128)(2,1)S(1)}, f32[2,192,1792]{2,...) custom-call(f32[8,128]{1,0:T(8,128)} %get-tuple-element.52.refs_0_, ...), custom_call_target="tpu_custom_call" | custom-call | tf_op jit(solution)/shard_map/update/pallas_call | solution.py:657
  419.0 10.9 %deliver.1 = (bf16[2,768,1792]{2,1,0:T(8,128)(2,1)}, bf16[2,768,1792]{2,1,0:T(8,128)(2,1)}, bf16[2,1792,768]{2,1,0:T(8,128)(2,1)}, f32[2,192,1792]{2,1,0:T(8,128...) custom-call(bf16[2,768,1792]{2,1,0:T(8,128)(2,1)S(1)} %get-tuple-ele, ...), custom_call_target="tpu_custom_call" | custom-call | tf_op jit(solution)/shard_map/deliver/pallas_call | solution.py:680
